TPU v7x, 8 devices: a whole 2x2x1 slice. The times are simulated.
8 devices in a mesh: dp: 2 (over z, y), tp: 4 (over x, core).
Axes of the slice: x: 2, y: 2, z: 1, core: 2. Of those that a mesh axis runs over, the one named last changes fastest.
Arguments:
- hidden: bfloat16 [512, 128], P(('dp', 'tp')), parts along dimension 0
- targets: int32 [512], P(('dp', 'tp')), parts along dimension 0
- loss_mask: int32 [512], P(('dp', 'tp')), parts along dimension 0
- ln_params: float32 [2, 128], replicated
- out_embed: bfloat16 [50304, 128], P('tp')
- ln_mom1: float32 [2, 128], replicated
- ln_mom2: float32 [2, 128], replicated
- embed_mom1: float32 [50304, 128], P('tp')
- embed_mom2: float32 [50304, 128], P('tp')
Outputs:
- output 1: float32 [512], P(('dp', 'tp')), parts along dimension 0
- output 2: float32 [2], P('dp'), parts along dimension 0
- output 3: bfloat16 [512, 128], P(('dp', 'tp')), parts along dimension 0
- output 4: float32 [4, 128], P('dp'), parts along dimension 0
- output 5: float32 [4, 128], P('dp'), parts along dimension 0
- output 6: float32 [4, 128], P('dp'), parts along dimension 0
- output 7: bfloat16 [100608, 128], P(('dp', 'tp')), parts along dimension 0
- output 8: float32 [100608, 128], P(('dp', 'tp')), parts along dimension 0
- output 9: float32 [100608, 128], P(('dp', 'tp')), parts along dimension 0
There are 2 independent parts. A program takes and returns all parts, laid end to end along the dimension named above; an argument that names none is the same for every part.
All inputs are finite; a program needn't handle non-finite values.
Results may differ from a plain program's by a relative error of at most 0.001.
Values are sent between devices in bfloat16 or wider.
A program may use at most 1 GiB of HBM per device.

v0:
```python
import jax
import jax.numpy as jnp
from jax import lax
from jax.sharding import PartitionSpec as P

LN_EPS = 1e-5
BETA_ONE = 0.9
BETA_TWO = 0.95
ADAM_EPS = 1e-8
LEARN_RATE = 1e-3
WEIGHT_DECAY = 0.1
ADAM_STEP = 10


def layer_norm(hidden, ln_params):
    rows_f32 = hidden.astype(jnp.float32)
    row_mean = jnp.mean(rows_f32, axis=-1, keepdims=True)
    centered = rows_f32 - row_mean
    row_var = jnp.mean(centered * centered, axis=-1, keepdims=True)
    normed = centered * lax.rsqrt(row_var + LN_EPS)
    return normed * ln_params[0] + ln_params[1]


def adam_step(param_val, grad_val, m_old, v_old, decay_rate):
    m_new = BETA_ONE * m_old + (1.0 - BETA_ONE) * grad_val
    v_new = BETA_TWO * v_old + (1.0 - BETA_TWO) * grad_val * grad_val
    m_hat = m_new / (1.0 - BETA_ONE ** ADAM_STEP)
    v_hat = v_new / (1.0 - BETA_TWO ** ADAM_STEP)
    new_param = param_val - LEARN_RATE * (m_hat / (jnp.sqrt(v_hat) + ADAM_EPS) + decay_rate * param_val)
    return new_param, m_new, v_new


def solution(mesh):
    row_spec = P(("dp", "tp"), None)
    tok_spec = P(("dp", "tp"))
    vocab_spec = P("tp", None)
    repl_spec = P()
    part_spec = P("dp", None)

    def device_step(hidden, targets, loss_mask, ln_params, out_embed, ln_mom1, ln_mom2, embed_mom1, embed_mom2):
        tok_local = hidden.shape[0]
        vocab_local = out_embed.shape[0]
        shard_idx = lax.axis_index("tp")
        x_norm, ln_vjp = jax.vjp(layer_norm, hidden, ln_params)
        x_full = lax.all_gather(x_norm.astype(jnp.bfloat16), "tp", tiled=True)
        tgt_full = lax.all_gather(targets, "tp", tiled=True)
        mask_full = lax.all_gather(loss_mask, "tp", tiled=True).astype(jnp.float32)
        logits = lax.dot_general(x_full, out_embed, (((1,), (1,)), ((), ())), preferred_element_type=jnp.float32)
        local_ids = jnp.arange(vocab_local, dtype=jnp.int32) + shard_idx * vocab_local
        is_target = local_ids[None, :] == tgt_full[:, None]
        local_max = jnp.max(logits, axis=1)
        local_sum = jnp.sum(jnp.exp(logits - local_max[:, None]), axis=1)
        tgt_logit = jnp.sum(jnp.where(is_target, logits, 0.0), axis=1)
        global_max = lax.pmax(local_max, "tp")
        shard_stats = lax.psum(jnp.stack([local_sum * jnp.exp(local_max - global_max), tgt_logit]), "tp")
        log_norm = global_max + jnp.log(shard_stats[0])
        loss_full = (log_norm - shard_stats[1]) * mask_full
        valid_count = jnp.sum(mask_full)
        mean_loss = (jnp.sum(loss_full) / valid_count).reshape(1)
        token_loss = lax.dynamic_slice_in_dim(loss_full, shard_idx * tok_local, tok_local)
        tok_scale = mask_full / valid_count
        d_logits = ((jnp.exp(logits - log_norm[:, None]) - is_target.astype(jnp.float32)) * tok_scale[:, None]).astype(jnp.bfloat16)
        d_embed = lax.dot_general(d_logits, x_full, (((0,), (0,)), ((), ())), preferred_element_type=jnp.float32)
        d_x_part = jnp.dot(d_logits, out_embed, preferred_element_type=jnp.float32)
        d_x = lax.psum_scatter(d_x_part, "tp", scatter_dimension=0, tiled=True)
        d_hidden, d_ln = ln_vjp(d_x)
        d_ln = lax.psum(d_ln, "tp")
        ln_new, ln_mom1_new, ln_mom2_new = adam_step(ln_params, d_ln, ln_mom1, ln_mom2, 0.0)
        embed_f, embed_mom1_new, embed_mom2_new = adam_step(out_embed.astype(jnp.float32), d_embed, embed_mom1, embed_mom2, WEIGHT_DECAY)
        return (token_loss, mean_loss, d_hidden, ln_new, ln_mom1_new, ln_mom2_new, embed_f.astype(jnp.bfloat16), embed_mom1_new, embed_mom2_new)

    return jax.shard_map(device_step, mesh=mesh, in_specs=(row_spec, tok_spec, tok_spec, repl_spec, vocab_spec, repl_spec, repl_spec, vocab_spec, vocab_spec), out_specs=(tok_spec, P("dp"), row_spec, part_spec, part_spec, part_spec, row_spec, row_spec, row_spec), check_vma=False)
```

profile of v0, /device:TPU:0, one launch (start us, length us, event | category | flops | bytes accessed | tf_op | source)
XLA Modules:
  0.0 108.3 jit_solution(7786976850159269448)
XLA Ops:
  7.2 0.0 reduce-scatter.2.cloned.1.call-start
  7.2 0.8 convert_reduce_fusion
  8.1 0.9 fusion.17
  9.0 1.2 %dynamic-slice = u32[1]{0:T(128)} dynamic-slice(u32[8]{0:T(128)} %constant.61, u32[]{:T(128)S(6)} %add.98), dynamic_slice_sizes={1} | dynamic-slice | bytes 12
  10.9 0.9 dynamic-update-slice.1
  11.7 0.8 dynamic-update-slice
  12.6 6.8 %all-reduce.4 = (s32[256]{0:T(256)S(1)}, s32[256]{0:T(256)S(1)}) all-reduce(s32[256]{0:T(256)S(1)} %dynamic-update-slice.1, s32[256]{0:T(256)S(1)} %dynamic-update-slice), channel_id=1, replica_groups=mesh['dp'=2,'tp'=4] {'tp'}, use_global_device_ids=true, to_apply=%add.3 | all-reduce | flops 512 | bytes 4096
  19.3 0.6 convert_reduce_fusion.1
  19.9 0.8 slice_bitcast_fusion.1
  20.7 0.8 fusion.15
  21.5 7.6 %all_gather.9 = bf16[256,128]{1,0:T(8,128)(2,1)S(1)} all-gather(bf16[64,128]{1,0:T(8,128)(2,1)S(1)} %fusion.15), channel_id=1, replica_groups=mesh['dp'=2,'tp'=4] {'tp'}, dimensions={0}, use_global_device_ids=true | all-gather | bytes 81920 | tf_op jit(solution)/shard_map/all_gather | solution.py:45
  29.1 8.7 %fusion.25 = (f32[256]{0:T(256)S(1)}, f32[256,12576]{0,1:T(8,128)}) fusion(bf16[256,128]{1,0:T(8,128)(2,1)S(1)} %all_gather.9, bf16[12576,128]{1,0:T(8,128)(2,1)} %param.13), kind=kOutput, calls=%fused_computation.51 | convolution fusion | flops 827399936 | bytes 16163840 | tf_op jit(solution)/shard_map/dot_general | solution.py:48
  37.8 5.6 %pmax.7 = f32[256]{0:T(256)S(1)} all-reduce(f32[256]{0:T(256)S(1)} %get-tuple-element.32), channel_id=1, replica_groups=mesh['dp'=2,'tp'=4] {'tp'}, use_global_device_ids=true, to_apply=%region_3.0 | all-reduce | flops 256 | bytes 2048 | tf_op jit(solution)/shard_map/pmax | solution.py:54
  43.5 10.1 %exponential_reduce_fusion = (f32[256]{0:T(256)S(1)}, f32[256]{0:T(256)S(1)}) fusion(f32[256,12576]{0,1:T(8,128)} %get-tuple-element.33, f32[256]{0:T(256)S(1)} %get-tuple-element.32, s32[256]{0:T(256)S(1)} %get-tuple-element.15, s32[12576]{0:T(1024)S(1)} %iota_add_fusion), kind=kLoop, calls=%fused_computation.6 | loop fusion | flops 16096768 | bytes 12932224 | tf_op jit(solution)/shard_map/reduce_sum | solution.py:52
  53.6 6.6 %psum.14 = f32[2,256]{1,0:T(2,128)S(1)} all-reduce(f32[2,256]{1,0:T(2,128)S(1)} %pad_maximum_fusion), channel_id=1, replica_groups=mesh['dp'=2,'tp'=4] {'tp'}, use_global_device_ids=true, to_apply=%region_6.7 | all-reduce | flops 512 | bytes 4096 | tf_op jit(solution)/shard_map/psum | solution.py:55
  60.1 1.2 %fusion.24 = (f32[]{:T(128)}, f32[256]{0:T(256)S(1)}, f32[256]{0:T(256)S(1)}, f32[256]{0:T(256)S(1)}) fusion(s32[256]{0:T(256)S(1)} %get-tuple-element.14, f32[256]{0:T(256)S(1)} %bitcast.21, f32[256]{0:T(256)S(1)} %pmax.7, f32[256]{0:T(256)S(1)} %bitcast.20, f32[]{:T(128)} %convert_reduce_fusion.1), kind=kLoop, calls=%fused_computation.50 | loop fusion | flops 1535 | bytes 7176 | tf_op jit(solution)/shard_map/reduce_sum | solution.py:59
  61.4 9.7 %fusion.3 = bf16[256,12576]{0,1:T(8,128)(2,1)S(1)} fusion(f32[256,12576]{0,1:T(8,128)} %get-tuple-element.33, f32[256]{0:T(256)S(1)} %get-tuple-element.29, f32[256]{0:T(256)S(1)} %get-tuple-element.26, s32[256]{0:T(256)S(1)} %get-tuple-element.15, s32[12576]{0:T(1024)S(1)} %iota_add_fusion), kind=kLoop, calls=%fused_computation.5 | loop fusion | flops 19316736 | bytes 19370112 | tf_op jit(solution)/shard_map/convert_element_type | solution.py:62
  71.1 2.7 %copy-done = bf16[256,12576]{0,1:T(8,128)(2,1)} copy-done((bf16[256,12576]{0,1:T(8,128)(2,1)}, bf16[256,12576]{0,1:T(8,128)(2,1)S(1)}, u32[]{:S(2)}) %copy-start) | copy-done | bytes 6438936
  73.8 0.0 copy-done.1
  73.8 2.7 %fusion.26 = f32[256,128]{1,0:T(8,128)} fusion(bf16[256,12576]{0,1:T(8,128)(2,1)S(1)} %fusion.3, bf16[12576,128]{1,0:T(8,128)(2,1)S(1)} %copy-done.1), kind=kOutput, calls=%fused_computation.52 | convolution fusion | flops 824180736 | bytes 9789440 | tf_op jit(solution)/shard_map/dot_general | solution.py:64
  76.5 0.0 reduce-scatter.2.cloned.1.call-update
  76.5 0.0 copy-start.2
  76.6 0.0 copy-start.3
  76.6 0.0 copy-start.4
  76.6 0.0 copy-start.5
  76.6 12.9 %fusion.6 = (bf16[12576,128]{1,0:T(8,128)(2,1)}, f32[12576,128]{1,0:T(8,128)}, f32[12576,128]{1,0:T(8,128)}) fusion(bf16[12576,128]{1,0:T(8,128)(2,1)S(1)} %copy-done.1, f32[12576,128]{1,0:T(8,128)} %param.16, f32[12576,128]{1,0:T(8,128)} %param.17, bf16[256,12576]{0,1:T(8,128)(2,1)} %copy-done, bf16[256,128]{1,0:T(8,128)(2,1)S(1)} %all_gather.9), kind=kOutput, calls=%fused_computation.12 | convolution fusion | flops 851546112 | bytes 38699008 | tf_op jit(solution)/shard_map/dot_general | solution.py:63
  90.8 0.6 dynamic_slice.3
  91.4 1.0 fusion.16
  92.4 5.7 %psum.15 = f32[2,128]{1,0:T(2,128)S(1)} all-reduce(f32[2,128]{1,0:T(2,128)S(1)} %pad_add_fusion), channel_id=1, replica_groups=mesh['dp'=2,'tp'=4] {'tp'}, use_global_device_ids=true, to_apply=%region_14.15 | all-reduce | flops 256 | bytes 2048 | tf_op jit(solution)/shard_map/psum | solution.py:67
  98.1 1.0 fusion.23
  99.0 0.7 add_convert_fusion
  99.7 0.6 multiply_subtract_fusion
  (18 shorter events, 0.1 us)
Async XLA Ops:
  7.2 84.2 %reduce-scatter.2.cloned.1.call-start = ((), (), s32[]{:S(2)}) async-start(), calls=%async_computation.1 | async-start | bytes 163840 | tf_op jit(solution)/shard_map/reduce_scatter | solution.py:65
  61.4 12.4 %copy-start.1 = (bf16[12576,128]{1,0:T(8,128)(2,1)S(1)}, bf16[12576,128]{1,0:T(8,128)(2,1)}, u32[]{:S(2)}) copy-start(bf16[12576,128]{1,0:T(8,128)(2,1)} %param.13) | copy-start | bytes 9658372
  71.1 2.7 %copy-start = (bf16[256,12576]{0,1:T(8,128)(2,1)}, bf16[256,12576]{0,1:T(8,128)(2,1)S(1)}, u32[]{:S(2)}) copy-start(bf16[256,12576]{0,1:T(8,128)(2,1)S(1)} %fusion.3) | copy-start | bytes 19316740
  76.5 14.9 %copy-start.2 = (bf16[64,128]{1,0:T(8,128)(2,1)S(1)}, bf16[64,128]{1,0:T(8,128)(2,1)}, u32[]{:S(2)}) copy-start(bf16[64,128]{1,0:T(8,128)(2,1)} %param.9) | copy-start | bytes 49156
  76.6 23.2 %copy-start.3 = (f32[2,128]{1,0:T(2,128)S(1)}, f32[2,128]{1,0:T(2,128)}, u32[]{:S(2)}) copy-start(f32[2,128]{1,0:T(2,128)} %param.12) | copy-start | bytes 3076
  76.6 23.2 %copy-start.4 = (f32[2,128]{1,0:T(2,128)S(1)}, f32[2,128]{1,0:T(2,128)}, u32[]{:S(2)}) copy-start(f32[2,128]{1,0:T(2,128)} %param.14) | copy-start | bytes 3076
  76.6 23.2 %copy-start.5 = (f32[2,128]{1,0:T(2,128)S(1)}, f32[2,128]{1,0:T(2,128)}, u32[]{:S(2)}) copy-start(f32[2,128]{1,0:T(2,128)} %param.15) | copy-start | bytes 3076
Sparse Core Ops, SparseCore 0:
  76.7 14.4 reduce-scatter.1
where the time goes:
time: 109 us; the launch traced here: 108 us
  blocking collectives  32.2 us (30%)
  other arithmetic  27.4 us (25%)
  matrix products  24.4 us (22%)
  between operations  17.3 us (16%)
  local copies, waits for them, and re-layouts  7.04 us (6%)
    dot_general x1, matrix products, device_step(): lax.dot_general(d_logits, x_full, (((0,), (0,)), ((), ())), preferred_ele...  12.9 us
    reduce_sum x1, other arithmetic, device_step(): local_sum = jnp.sum(jnp.exp(logits - local_max[:, None]), axis=1)  10.1 us
    convert_element_type x1, other arithmetic, device_step(): ((jnp.exp(logits - log_norm[:, None]) - is_target.astype(jnp.float32)) *...  9.68 us
    dot_general x1, matrix products, device_step(): lax.dot_general(x_full, out_embed, (((1,), (1,)), ((), ())), preferred_el...  8.75 us
    all_gather x1, blocking collectives, device_step(): x_full = lax.all_gather(x_norm.astype(jnp.bfloat16), 'tp', tiled=True)  7.56 us
    unnamed x1, blocking collectives  6.75 us
    psum x1, blocking collectives, device_step(): lax.psum(jnp.stack([local_sum * jnp.exp(local_max - global_max), tgt_logi...  6.56 us
    unnamed x17, local copies, waits for them, and re-layouts  5.68 us
  transfers between devices with their start and end apart: 1, of which 0 were waited for; matrix products, arithmetic and copies ran while one was open for 12% of the time, Pallas kernels for 0%

commit v1 on v0

v1 whole, which is shorter than its diff:
```python
import functools

import jax
import jax.numpy as jnp
from jax import lax
from jax.experimental import pallas as pl
from jax.experimental.pallas import tpu as pltpu
from jax.sharding import PartitionSpec as P

LN_EPS = 1e-5
BETA_ONE = 0.9
BETA_TWO = 0.95
ADAM_EPS = 1e-8
LEARN_RATE = 1e-3
WEIGHT_DECAY = 0.1
ADAM_STEP = 10
LOG2E = 1.4426950408889634
TINY = 1e-37
SUB = 128
MESH = pl.DeviceIdType.MESH
F32 = jnp.float32
BF16 = jnp.bfloat16


def block_plan(rows):
    subs = rows // SUB
    per = next(k for k in (14, 7, 8, 6, 4, 3, 2, 1) if subs % k == 0)
    return subs // per, per, rows - subs * SUB


def adam_const():
    one = 1.0 - BETA_ONE ** ADAM_STEP
    two = 1.0 - BETA_TWO ** ADAM_STEP
    root = two ** 0.5
    return LEARN_RATE * root / one, ADAM_EPS * root


def adam(param, grad, m_old, v_old, decay):
    scale, eps = adam_const()
    m_new = BETA_ONE * m_old + (1.0 - BETA_ONE) * grad
    v_new = BETA_TWO * v_old + ((1.0 - BETA_TWO) * grad) * grad
    root = v_new * lax.rsqrt(v_new + TINY)
    kept = param if decay == 0.0 else (1.0 - LEARN_RATE * decay) * param
    return kept - (scale * m_new) / (root + eps), m_new, v_new


def forward_kernel(n, hid_ref, tgt_ref, msk_ref, ln_ref, lm_ref, lv_ref, e_hbm, m_hbm, v_hbm,
                   e_v, m_v, v_v, dz_v, x_v, tok_o, mean_o, dh_o, ln_o, lmo, lvo,
                   hid_s, tgt_s, msk_s, xhat_s, rstd_s, ebuf, mbuf, et_s, st_tx, st_rx, pk_tx, pk_rx,
                   load_sem, in_send, in_recv, st_send, st_recv, pk_send, pk_recv):
    me = lax.axis_index("tp")
    rows, dim = e_v.shape
    local = hid_ref.shape[0]
    toks = n * local
    nblk, per, tail = block_plan(rows)
    blk = per * SUB

    barrier = pltpu.get_barrier_semaphore()
    for d in range(1, n):
        pl.semaphore_signal(barrier, inc=1, device_id={"tp": lax.rem(me + d, n)}, device_id_type=MESH)
    e_copy = pltpu.make_async_copy(e_hbm, e_v, load_sem.at[0])
    m_copy = pltpu.make_async_copy(m_hbm, m_v, load_sem.at[1])
    v_copy = pltpu.make_async_copy(v_hbm, v_v, load_sem.at[2])
    e_copy.start()
    pl.semaphore_wait(barrier, n - 1)

    gathers = []
    for d in range(1, n):
        for k, (src, dst) in enumerate(((hid_ref, hid_s), (tgt_ref, tgt_s), (msk_ref, msk_s))):
            copy = pltpu.make_async_remote_copy(
                src_ref=src, dst_ref=dst.at[me], send_sem=in_send.at[k, d - 1], recv_sem=in_recv.at[k, d - 1],
                device_id={"tp": lax.rem(me + d, n)}, device_id_type=MESH)
            copy.start()
            gathers.append(copy)
    hid_s[me] = hid_ref[...]
    tgt_s[me] = tgt_ref[...]
    msk_s[me] = msk_ref[...]
    e_copy.wait()
    m_copy.start()
    v_copy.start()

    def turn(base, size):
        et_s[:, pl.ds(base, size)] = e_v[pl.ds(base, size), :].T

    def turn_block(i, carry):
        turn(pl.multiple_of(i * blk, blk), blk)
        return carry

    lax.fori_loop(0, nblk, turn_block, 0)
    if tail:
        turn(nblk * blk, tail)

    for copy in gathers:
        copy.wait_recv()

    hid = hid_s[...].reshape(toks, dim).astype(F32)
    cent = hid - jnp.mean(hid, axis=-1, keepdims=True)
    rstd = lax.rsqrt(jnp.mean(cent * cent, axis=-1, keepdims=True) + LN_EPS)
    xhat = cent * rstd
    x_f = xhat * ln_ref[0:1, :] + ln_ref[1:2, :]
    x_v[...] = x_f.astype(BF16)
    xhat_s[...] = xhat
    rstd_s[...] = jnp.broadcast_to(rstd, (toks, dim))
    tgt = jnp.concatenate([tgt_s[j] for j in range(n)], axis=1)
    msk = jnp.concatenate([msk_s[j] for j in range(n)], axis=1).astype(F32)
    count = jnp.sum(msk, axis=1, keepdims=True)
    scale = msk / count
    rel = tgt - me * rows

    def fwd(base, slot, subs, size, top, total):
        z = lax.dot_general(e_v[pl.ds(base, subs * size), :], x_v[...], (((1,), (1,)), ((), ())),
                            preferred_element_type=F32)
        for k in range(subs):
            zk = z[k * size:(k + 1) * size].reshape(size // 8, 8, toks)
            new = jnp.maximum(top, jnp.max(zk, axis=0))
            ek = jnp.exp2((zk - new[None]) * LOG2E)
            ebuf[pl.ds(base + k * size, size), :] = ek.reshape(size, toks)
            mbuf[slot + k] = new
            total = total * jnp.exp2((top - new) * LOG2E) + jnp.sum(ek, axis=0)
            top = new
        return top, total

    def fwd_block(i, carry):
        return fwd(pl.multiple_of(i * blk, blk), i * per, per, SUB, *carry)

    carry = (jnp.full((8, toks), -jnp.inf, F32), jnp.zeros((8, toks), F32))
    carry = lax.fori_loop(0, nblk, fwd_block, carry)
    if tail:
        carry = fwd(nblk * blk, nblk * per, 1, tail, *carry)
    top8, sum8 = carry
    top = jnp.max(top8, axis=0, keepdims=True)
    total = jnp.sum(sum8 * jnp.exp2((top8 - top) * LOG2E), axis=0, keepdims=True)
    st_tx[0:1, :] = top
    st_tx[1:2, :] = total
    st_rx[me] = st_tx[...]
    stats = []
    for d in range(1, n):
        copy = pltpu.make_async_remote_copy(
            src_ref=st_tx, dst_ref=st_rx.at[me], send_sem=st_send.at[d - 1], recv_sem=st_recv.at[d - 1],
            device_id={"tp": lax.rem(me + d, n)}, device_id_type=MESH)
        copy.start()
        stats.append(copy)

    iota = lax.broadcasted_iota(jnp.int32, (SUB, toks), 0)

    def pick(base, subs, size, acc):
        hot = jnp.concatenate(
            [(iota[:size] == rel - (base + k * size)).astype(F32).astype(BF16) for k in range(subs)], axis=0)
        return acc + jnp.dot(et_s[:, pl.ds(base, subs * size)], hot, preferred_element_type=F32)

    def pick_block(i, acc):
        return pick(pl.multiple_of(i * blk, blk), per, SUB, acc)

    rows_t = lax.fori_loop(0, nblk, pick_block, jnp.zeros((dim, toks), F32))
    if tail:
        rows_t = pick(nblk * blk, 1, tail, rows_t)
    tgt_z = jnp.sum(x_v[...].astype(F32).T * rows_t, axis=0, keepdims=True)
    inside = (rel >= 0) & (rel < rows)
    tgt_z = jnp.where(inside, tgt_z, 0.0)

    for copy in stats:
        copy.wait_recv()
    tops = [st_rx[j, 0:1, :] for j in range(n)]
    top = functools.reduce(jnp.maximum, tops)
    total = sum(st_rx[j, 1:2, :] * jnp.exp2((tops[j] - top) * LOG2E) for j in range(n))
    lse = top + jnp.log(total)
    hot_val = (jnp.exp2((tgt_z - lse) * LOG2E) - 1.0) * scale

    def back(base, slot, subs, size, acc):
        for k in range(subs):
            fac = jnp.exp2((mbuf[slot + k] - lse) * LOG2E) * scale
            ek = ebuf[pl.ds(base + k * size, size), :].reshape(size // 8, 8, toks)
            dz = (ek * fac[None]).reshape(size, toks)
            dz = jnp.where(iota[:size] == rel - (base + k * size), hot_val, dz)
            dz_v[pl.ds(base + k * size, size), :] = dz.astype(BF16)
        return acc + jnp.dot(et_s[:, pl.ds(base, subs * size)], dz_v[pl.ds(base, subs * size), :],
                             preferred_element_type=F32)

    def back_block(i, acc):
        return back(pl.multiple_of(i * blk, blk), i * per, per, SUB, acc)

    dx_t = lax.fori_loop(0, nblk, back_block, jnp.zeros((dim, toks), F32))
    if tail:
        dx_t = back(nblk * blk, nblk * per, 1, tail, dx_t)
    dx = dx_t.T
    xhat = xhat_s[...]
    extra = jnp.concatenate(
        [jnp.sum(dx * xhat, axis=0, keepdims=True), jnp.sum(dx, axis=0, keepdims=True)]
        + [tgt_z[:, c * dim:(c + 1) * dim] for c in range(toks // dim)]
        + [jnp.zeros((6 - toks // dim, dim), F32)], axis=0)
    for j in range(n):
        pk_tx[j, 0:local, :] = dx[j * local:(j + 1) * local]
        pk_tx[j, local:local + 8, :] = extra
    parts = []
    for d in range(1, n):
        peer = lax.rem(me + d, n)
        copy = pltpu.make_async_remote_copy(
            src_ref=pk_tx.at[peer], dst_ref=pk_rx.at[me], send_sem=pk_send.at[d - 1], recv_sem=pk_recv.at[d - 1],
            device_id={"tp": peer}, device_id_type=MESH)
        copy.start()
        parts.append(copy)
    pk_rx[me] = pk_tx[me]
    for copy in parts:
        copy.wait_recv()

    dx = sum(pk_rx[j, 0:local, :] for j in range(n))
    extra = sum(pk_rx[j, local:local + 8, :] for j in range(n))
    tgt_z = jnp.concatenate([extra[2 + c:3 + c] for c in range(toks // dim)], axis=1)
    loss = (lse - tgt_z) * msk
    mean_o[...] = jnp.sum(loss, axis=1, keepdims=True) / count
    tok_o[...] = sum(jnp.where(me == j, loss[:, j * local:(j + 1) * local], 0.0) for j in range(n))
    own = pl.ds(pl.multiple_of(me * local, local), local)
    xhat = xhat_s[own, :]
    dxh = dx * ln_ref[0:1, :]
    dh = rstd_s[own, :] * (dxh - jnp.mean(dxh, axis=-1, keepdims=True)
                           - xhat * jnp.mean(dxh * xhat, axis=-1, keepdims=True))
    dh_o[...] = dh.astype(BF16)
    p_new, m_new, v_new = adam(ln_ref[...], extra[0:2], lm_ref[...], lv_ref[...], 0.0)
    ln_o[...] = p_new
    lmo[...] = m_new
    lvo[...] = v_new
    m_copy.wait()
    v_copy.wait()
    for copy in gathers + stats + parts:
        copy.wait_send()


def update_kernel(e_v, m_v, v_v, dz_v, x_v, *rest):
    small_in, big_out, small_out, (e_s, m_s, v_s, sem, small_sem) = rest[:6], rest[6:9], rest[9:15], rest[15:]
    rows, dim = e_v.shape
    nblk, per, tail = block_plan(rows)
    blk = per * SUB
    smalls = [pltpu.make_async_copy(a, b, small_sem.at[k]) for k, (a, b) in enumerate(zip(small_in, small_out))]
    for copy in smalls:
        copy.start()
    stages = (e_s, m_s, v_s)

    def step(base, size):
        sl = pl.ds(base, size)
        g = jnp.dot(dz_v[sl, :], x_v[...], preferred_element_type=F32)
        p_new, m_new, v_new = adam(e_v[sl, :].astype(F32), g, m_v[sl, :], v_v[sl, :], WEIGHT_DECAY)
        e_s[sl, :] = p_new.astype(BF16)
        m_s[sl, :] = m_new
        v_s[sl, :] = v_new
        for k in range(3):
            pltpu.make_async_copy(stages[k].at[sl], big_out[k].at[sl], sem.at[k]).start()

    def step_block(i, carry):
        step(pl.multiple_of(i * blk, blk), blk)
        return carry

    lax.fori_loop(0, nblk, step_block, 0)
    if tail:
        step(nblk * blk, tail)
    for k in range(3):
        pltpu.make_async_copy(stages[k], big_out[k], sem.at[k]).wait()
    for copy in smalls:
        copy.wait()


def solution(mesh):
    n = mesh.shape["tp"]
    row_spec = P(("dp", "tp"), None)
    tok_spec = P(("dp", "tp"))
    vocab_spec = P("tp", None)
    repl_spec = P()
    part_spec = P("dp", None)
    vmem = pl.BlockSpec(memory_space=pltpu.VMEM)
    anyw = pl.BlockSpec(memory_space=pltpu.HBM)

    def device_step(hidden, targets, loss_mask, ln_params, out_embed, ln_mom1, ln_mom2, embed_mom1, embed_mom2):
        local, dim = hidden.shape
        rows = out_embed.shape[0]
        toks = n * local
        nblk, per, tail = block_plan(rows)
        pad = -(-rows // 128) * 128
        big = [pltpu.VMEM((rows, dim), BF16), pltpu.VMEM((rows, dim), F32), pltpu.VMEM((rows, dim), F32),
               pltpu.VMEM((rows, toks), BF16), pltpu.VMEM((toks, dim), BF16)]
        small = [((1, local), F32), ((1, 1), F32), ((local, dim), BF16), ((2, dim), F32), ((2, dim), F32),
                 ((2, dim), F32)]
        dma = pltpu.SemaphoreType.DMA
        mids = pl.pallas_call(
            functools.partial(forward_kernel, n),
            name="forward",
            out_shape=big + [pltpu.VMEM(*s) for s in small],
            in_specs=[vmem] * 6 + [anyw] * 3,
            out_specs=[vmem] * 11,
            scratch_shapes=[
                pltpu.VMEM((n, local, dim), BF16), pltpu.VMEM((n, 1, local), jnp.int32),
                pltpu.VMEM((n, 1, local), jnp.int32), pltpu.VMEM((toks, dim), F32), pltpu.VMEM((toks, dim), F32),
                pltpu.VMEM((rows, toks), F32), pltpu.VMEM((nblk * per + 1, 8, toks), F32),
                pltpu.VMEM((dim, pad), BF16),
                pltpu.VMEM((2, toks), F32), pltpu.VMEM((n, 2, toks), F32),
                pltpu.VMEM((n, local + 8, dim), F32), pltpu.VMEM((n, local + 8, dim), F32),
                dma((3,)), dma((3, n - 1)), dma((3, n - 1)), dma((n - 1,)), dma((n - 1,)), dma((n - 1,)),
                dma((n - 1,)),
            ],
            compiler_params=pltpu.CompilerParams(
                collective_id=0, has_side_effects=True, vmem_limit_bytes=24 << 20),
        )(hidden, targets.reshape(1, local), loss_mask.reshape(1, local), ln_params, ln_mom1, ln_mom2,
          out_embed, embed_mom1, embed_mom2)
        hbm = lambda shape, dtype: jax.ShapeDtypeStruct(shape, dtype)
        outs = pl.pallas_call(
            update_kernel,
            name="update",
            out_shape=[hbm((rows, dim), BF16), hbm((rows, dim), F32), hbm((rows, dim), F32)]
            + [hbm(*s) for s in small],
            in_specs=[vmem] * 11,
            out_specs=[anyw] * 9,
            scratch_shapes=[pltpu.VMEM((rows, dim), BF16), pltpu.VMEM((rows, dim), F32), pltpu.VMEM((rows, dim), F32),
                            dma((3,)), dma((6,))],
            compiler_params=pltpu.CompilerParams(vmem_limit_bytes=20 << 20),
        )(*[pltpu.with_memory_space_constraint(a, pltpu.VMEM) for a in mids])
        e_new, m_new, v_new, tok, mean, dh, ln_new, lm_new, lv_new = outs
        return (tok.reshape(local), mean.reshape(1), dh, ln_new, lm_new, lv_new, e_new, m_new, v_new)

    return jax.shard_map(device_step, mesh=mesh, in_specs=(row_spec, tok_spec, tok_spec, repl_spec, vocab_spec, repl_spec, repl_spec, vocab_spec, vocab_spec), out_specs=(tok_spec, P("dp"), row_spec, part_spec, part_spec, part_spec, row_spec, row_spec, row_spec), check_vma=False)
```

time: 109 us -> 36.9 us (0.34)
  blocking collectives: 32.2 us -> 0 us
  Pallas kernels: 0 us -> 29.9 us
  other arithmetic: 27.4 us -> 0 us
  matrix products: 24.4 us -> 0 us
  between operations: 17.3 us -> 0.67 us
    pallas_call x0 -> x2, Pallas kernels: none -> 29.9 us  [the longest x1 22.7 us: device_step(): pl.pallas_call(functools.partial(forward_kernel, n), name='forward', out_...]
    dot_general x3 -> x0, matrix products: 24.4 us -> none  [the longest x1 12.9 us: device_step(): lax.dot_general(d_logits, x_full, (((0,), (0,)), ((), ())), preferred_ele...]
    reduce_sum x7 -> x0, other arithmetic: 15.6 us -> none  [the longest x1 10.1 us: device_step(): local_sum = jnp.sum(jnp.exp(logits - local_max[:, None]), axis=1)]
    psum x2 -> x0, blocking collectives: 12.2 us -> none  [the longest x1 6.56 us: device_step(): lax.psum(jnp.stack([local_sum * jnp.exp(local_max - global_max), tgt_logi...]
    convert_element_type x3 -> x0, other arithmetic: 11.2 us -> none  [the longest x1 9.68 us: device_step(): ((jnp.exp(logits - log_norm[:, None]) - is_target.astype(jnp.float32)) *...]
    all_gather x1 -> x0, blocking collectives: 7.56 us -> none  [device_step(): x_full = lax.all_gather(x_norm.astype(jnp.bfloat16), 'tp', tiled=True)]
    unnamed x1 -> x0, blocking collectives: 6.75 us -> none
    pmax x1 -> x0, blocking collectives: 5.63 us -> none  [device_step(): global_max = lax.pmax(local_max, 'tp')]
  transfers between devices with their start and end apart: 1 -> 0, of which waited for: 0 -> 0; matrix products, arithmetic and copies ran while one was open for 12% -> 0% of each run, Pallas kernels for 0% -> 0%
where the time goes in v1:
time: 36.9 us; the launch traced here: 36.6 us
  Pallas kernels  29.9 us (81%)
  local copies, waits for them, and re-layouts  5.96 us (16%)
  between operations  0.67 us (2%)
    pallas_call x1, Pallas kernels, device_step(): pl.pallas_call(functools.partial(forward_kernel, n), name='forward', out_...  22.7 us
    pallas_call x1, Pallas kernels, device_step(): pl.pallas_call(update_kernel, name='update', out_shape=[hbm((rows, dim),...  7.27 us
    unnamed x14, local copies, waits for them, and re-layouts  5.96 us

profile of v1, /device:TPU:0, one launch (start us, length us, event | category | flops | bytes accessed | tf_op | source)
XLA Modules:
  0.0 36.6 jit_solution(2407921296814597376)
XLA Ops:
  0.6 0.0 copy-start
  0.7 1.9 %copy-done = bf16[12576,128]{1,0:T(8,128)(2,1)S(1)} copy-done((bf16[12576,128]{1,0:T(8,128)(2,1)S(1)}, bf16[12576,128]{1,0:T(8,128)(2,1)}, u32[]{:S(2)}) %copy-start) | copy-done | bytes 3219480
  2.6 0.0 copy-start.1
  2.6 0.7 %copy-done.1 = bf16[64,128]{1,0:T(8,128)(2,1)S(1)} copy-done((bf16[64,128]{1,0:T(8,128)(2,1)S(1)}, bf16[64,128]{1,0:T(8,128)(2,1)}, u32[]{:S(2)}) %copy-start.1) | copy-done | bytes 16408
  3.3 0.0 copy-start.2
  3.3 0.7 %copy-done.2 = f32[2,128]{1,0:T(2,128)S(1)} copy-done((f32[2,128]{1,0:T(2,128)S(1)}, f32[2,128]{1,0:T(2,128)}, u32[]{:S(2)}) %copy-start.2) | copy-done | bytes 1048
  4.0 0.0 copy-start.3
  4.0 0.7 %copy-done.3 = f32[2,128]{1,0:T(2,128)S(1)} copy-done((f32[2,128]{1,0:T(2,128)S(1)}, f32[2,128]{1,0:T(2,128)}, u32[]{:S(2)}) %copy-start.3) | copy-done | bytes 1048
  4.6 0.0 copy-start.4
  4.6 0.7 %copy-done.4 = f32[2,128]{1,0:T(2,128)S(1)} copy-done((f32[2,128]{1,0:T(2,128)S(1)}, f32[2,128]{1,0:T(2,128)}, u32[]{:S(2)}) %copy-start.4) | copy-done | bytes 1048
  5.3 0.0 copy-start.5
  5.3 0.7 %copy-done.5 = s32[64]{0:T(128)S(1)} copy-done((s32[64]{0:T(128)S(1)}, s32[64]{0:T(128)}, u32[]{:S(2)}) %copy-start.5) | copy-done | bytes 280
  6.0 0.0 copy-start.6
  6.0 0.7 %copy-done.6 = s32[64]{0:T(128)S(1)} copy-done((s32[64]{0:T(128)S(1)}, s32[64]{0:T(128)}, u32[]{:S(2)}) %copy-start.6) | copy-done | bytes 280
  6.6 22.7 %forward.1 = (bf16[12576,128]{1,0:T(8,128)(2,1)S(1)}, f32[12576,128]{1,0:T(8,128)S(1)}, f32[12576,128]{1,0:T(8,128)S(1)}, bf16[12576,256]{1,0:T(8,128)(2,1)S(1)}...) custom-call(bf16[64,128]{1,0:T(8,128)(2,1)S(1)} %copy-done.1, ...), custom_call_target="tpu_custom_call" | custom-call | tf_op jit(solution)/shard_map/forward/pallas_call | solution.py:282
  29.3 7.3 %update.1 = (bf16[12576,128]{1,0:T(8,128)(2,1)}, f32[12576,128]{1,0:T(8,128)}, f32[12576,128]{1,0:T(8,128)}, f32[1,64]{1,0:T(1,128)}, f32[1,1]{1,0:T(1,128)}, /*...) custom-call(bf16[12576,128]{1,0:T(8,128)(2,1)S(1)} %get-tuple-element.29.e_v, ...), custom_call_target="tpu_custom_call" | custom-call | tf_op jit(solution)/shard_map/update/pallas_call | solution.py:303
Async XLA Ops:
  0.6 1.9 %copy-start = (bf16[12576,128]{1,0:T(8,128)(2,1)S(1)}, bf16[12576,128]{1,0:T(8,128)(2,1)}, u32[]{:S(2)}) copy-start(bf16[12576,128]{1,0:T(8,128)(2,1)} %e_hbm.1) | copy-start | bytes 9658372
  2.6 0.7 %copy-start.1 = (bf16[64,128]{1,0:T(8,128)(2,1)S(1)}, bf16[64,128]{1,0:T(8,128)(2,1)}, u32[]{:S(2)}) copy-start(bf16[64,128]{1,0:T(8,128)(2,1)} %hid_ref.1) | copy-start | bytes 49156
  3.3 0.7 %copy-start.2 = (f32[2,128]{1,0:T(2,128)S(1)}, f32[2,128]{1,0:T(2,128)}, u32[]{:S(2)}) copy-start(f32[2,128]{1,0:T(2,128)} %ln_ref.1) | copy-start | bytes 3076
  4.0 0.7 %copy-start.3 = (f32[2,128]{1,0:T(2,128)S(1)}, f32[2,128]{1,0:T(2,128)}, u32[]{:S(2)}) copy-start(f32[2,128]{1,0:T(2,128)} %lm_ref.1) | copy-start | bytes 3076
  4.6 0.7 %copy-start.4 = (f32[2,128]{1,0:T(2,128)S(1)}, f32[2,128]{1,0:T(2,128)}, u32[]{:S(2)}) copy-start(f32[2,128]{1,0:T(2,128)} %lv_ref.1) | copy-start | bytes 3076
  5.3 0.7 %copy-start.5 = (s32[64]{0:T(128)S(1)}, s32[64]{0:T(128)}, u32[]{:S(2)}) copy-start(s32[64]{0:T(128)} %param.10) | copy-start | bytes 772
  6.0 0.7 %copy-start.6 = (s32[64]{0:T(128)S(1)}, s32[64]{0:T(128)}, u32[]{:S(2)}) copy-start(s32[64]{0:T(128)} %param.11) | copy-start | bytes 772

commit v2 on v1

--- a/solution.py
+++ b/solution.py
@@ -44,9 +44,9 @@
     return kept - (scale * m_new) / (root + eps), m_new, v_new
 
 
-def forward_kernel(n, hid_ref, tgt_ref, msk_ref, ln_ref, lm_ref, lv_ref, e_hbm, m_hbm, v_hbm,
+def forward_kernel(n, hid_hbm, tgt_hbm, msk_hbm, ln_hbm, lm_hbm, lv_hbm, e_hbm, m_hbm, v_hbm,
                    e_v, m_v, v_v, dz_v, x_v, tok_o, mean_o, dh_o, ln_o, lmo, lvo,
-                   hid_s, tgt_s, msk_s, xhat_s, rstd_s, ebuf, mbuf, et_s, st_tx, st_rx, pk_tx, pk_rx,
+                   hid_ref, tgt_ref, msk_ref, ln_ref, lm_ref, lv_ref, hid_s, tgt_s, msk_s, xhat_s, rstd_s, ebuf, mbuf, et_s, st_tx, st_rx, pk_tx, pk_rx,
                    load_sem, in_send, in_recv, st_send, st_recv, pk_send, pk_recv):
     me = lax.axis_index("tp")
     rows, dim = e_v.shape
@@ -58,10 +58,17 @@
     barrier = pltpu.get_barrier_semaphore()
     for d in range(1, n):
         pl.semaphore_signal(barrier, inc=1, device_id={"tp": lax.rem(me + d, n)}, device_id_type=MESH)
+    firsts = [pltpu.make_async_copy(a, b, load_sem.at[3 + k]) for k, (a, b) in enumerate((
+        (hid_hbm, hid_ref), (tgt_hbm, tgt_ref), (msk_hbm, msk_ref), (ln_hbm, ln_ref), (lm_hbm, lm_ref),
+        (lv_hbm, lv_ref)))]
+    for copy in firsts:
+        copy.start()
     e_copy = pltpu.make_async_copy(e_hbm, e_v, load_sem.at[0])
     m_copy = pltpu.make_async_copy(m_hbm, m_v, load_sem.at[1])
     v_copy = pltpu.make_async_copy(v_hbm, v_v, load_sem.at[2])
     e_copy.start()
+    for copy in firsts:
+        copy.wait()
     pl.semaphore_wait(barrier, n - 1)
 
     gathers = []
@@ -283,22 +290,25 @@
             functools.partial(forward_kernel, n),
             name="forward",
             out_shape=big + [pltpu.VMEM(*s) for s in small],
-            in_specs=[vmem] * 6 + [anyw] * 3,
+            in_specs=[anyw] * 9,
             out_specs=[vmem] * 11,
             scratch_shapes=[
+                pltpu.VMEM((local, dim), BF16), pltpu.VMEM((1, local), jnp.int32), pltpu.VMEM((1, local), jnp.int32),
+                pltpu.VMEM((2, dim), F32), pltpu.VMEM((2, dim), F32), pltpu.VMEM((2, dim), F32),
                 pltpu.VMEM((n, local, dim), BF16), pltpu.VMEM((n, 1, local), jnp.int32),
                 pltpu.VMEM((n, 1, local), jnp.int32), pltpu.VMEM((toks, dim), F32), pltpu.VMEM((toks, dim), F32),
                 pltpu.VMEM((rows, toks), F32), pltpu.VMEM((nblk * per + 1, 8, toks), F32),
                 pltpu.VMEM((dim, pad), BF16),
                 pltpu.VMEM((2, toks), F32), pltpu.VMEM((n, 2, toks), F32),
                 pltpu.VMEM((n, local + 8, dim), F32), pltpu.VMEM((n, local + 8, dim), F32),
-                dma((3,)), dma((3, n - 1)), dma((3, n - 1)), dma((n - 1,)), dma((n - 1,)), dma((n - 1,)),
+                dma((9,)), dma((3, n - 1)), dma((3, n - 1)), dma((n - 1,)), dma((n - 1,)), dma((n - 1,)),
                 dma((n - 1,)),
             ],
             compiler_params=pltpu.CompilerParams(
                 collective_id=0, has_side_effects=True, vmem_limit_bytes=24 << 20),
-        )(hidden, targets.reshape(1, local), loss_mask.reshape(1, local), ln_params, ln_mom1, ln_mom2,
-          out_embed, embed_mom1, embed_mom2)
+        )(*[pltpu.with_memory_space_constraint(a, pltpu.HBM) for a in (
+            hidden, targets.reshape(1, local), loss_mask.reshape(1, local), ln_params, ln_mom1, ln_mom2,
+            out_embed, embed_mom1, embed_mom2)])
         hbm = lambda shape, dtype: jax.ShapeDtypeStruct(shape, dtype)
         outs = pl.pallas_call(
             update_kernel,

time: 36.9 us -> 30.9 us (0.84)
  local copies, waits for them, and re-layouts: 5.96 us -> 0 us
    unnamed x14 -> x0, local copies, waits for them, and re-layouts: 5.96 us -> none
where the time goes in v2:
time: 30.9 us; the launch traced here: 30.7 us
  Pallas kernels  30 us (97%)
  between operations  0.65 us (2%)
    pallas_call x1, Pallas kernels, device_step(): pl.pallas_call(functools.partial(forward_kernel, n), name='forward', out_...  22.8 us
    pallas_call x1, Pallas kernels, device_step(): pl.pallas_call(update_kernel, name='update', out_shape=[hbm((rows, dim),...  7.21 us

profile of v2, /device:TPU:0, one launch (start us, length us, event | category | flops | bytes accessed | tf_op | source)
XLA Modules:
  0.0 30.7 jit_solution(3459698850144202221)
XLA Ops:
  0.6 22.8 %forward.1 = (bf16[12576,128]{1,0:T(8,128)(2,1)S(1)}, f32[12576,128]{1,0:T(8,128)S(1)}, f32[12576,128]{1,0:T(8,128)S(1)}, bf16[12576,256]{1,0:T(8,128)(2,1)S(1)}...) custom-call(bf16[64,128]{1,0:T(8,128)(2,1)} %hid_hbm.1, ...), custom_call_target="tpu_custom_call" | custom-call | tf_op jit(solution)/shard_map/forward/pallas_call | solution.py:289
  23.4 7.2 %update.1 = (bf16[12576,128]{1,0:T(8,128)(2,1)}, f32[12576,128]{1,0:T(8,128)}, f32[12576,128]{1,0:T(8,128)}, f32[1,64]{1,0:T(1,128)}, f32[1,1]{1,0:T(1,128)}, /*...) custom-call(bf16[12576,128]{1,0:T(8,128)(2,1)S(1)} %get-tuple-element.29.e_v, ...), custom_call_target="tpu_custom_call" | custom-call | tf_op jit(solution)/shard_map/update/pallas_call | solution.py:313

commit v3 on v2

--- a/solution.py
+++ b/solution.py
@@ -45,9 +45,10 @@
 
 
 def forward_kernel(n, hid_hbm, tgt_hbm, msk_hbm, ln_hbm, lm_hbm, lv_hbm, e_hbm, m_hbm, v_hbm,
-                   e_v, m_v, v_v, dz_v, x_v, tok_o, mean_o, dh_o, ln_o, lmo, lvo,
-                   hid_ref, tgt_ref, msk_ref, ln_ref, lm_ref, lv_ref, hid_s, tgt_s, msk_s, xhat_s, rstd_s, ebuf, mbuf, et_s, st_tx, st_rx, pk_tx, pk_rx,
-                   load_sem, in_send, in_recv, st_send, st_recv, pk_send, pk_recv):
+                   e_v, m_v, v_v, dz_v, x_v, xh_o, rs_o, lse_o, msk_o, ln_ref, lm_ref, lv_ref, *rest):
+    pks, rest = rest[:n], rest[n:]
+    (hid_ref, tgt_ref, msk_ref, hid_s, tgt_s, msk_s, xhat_s, rstd_s, ebuf, mbuf, et_s, st_tx, st_rx, pk_tx,
+     load_sem, in_send, in_recv, st_send, st_recv) = rest
     me = lax.axis_index("tp")
     rows, dim = e_v.shape
     local = hid_ref.shape[0]
@@ -131,7 +132,8 @@
         return fwd(pl.multiple_of(i * blk, blk), i * per, per, SUB, *carry)
 
     carry = (jnp.full((8, toks), -jnp.inf, F32), jnp.zeros((8, toks), F32))
-    carry = lax.fori_loop(0, nblk, fwd_block, carry)
+    for i in range(nblk):
+        carry = fwd(i * blk, i * per, per, SUB, *carry)
     if tail:
         carry = fwd(nblk * blk, nblk * per, 1, tail, *carry)
     top8, sum8 = carry
@@ -173,20 +175,34 @@
     lse = top + jnp.log(total)
     hot_val = (jnp.exp2((tgt_z - lse) * LOG2E) - 1.0) * scale
 
+    hot16 = jnp.broadcast_to(hot_val, (16, toks)).astype(BF16)[None]
+    zero = jnp.zeros((16, toks), jnp.int32)
+    iota16 = lax.broadcasted_iota(jnp.int32, (SUB, toks), 0).astype(jnp.int16).reshape(SUB // 16, 16, toks)
+    near = jnp.where(inside, rel, -15000)
+
     def back(base, slot, subs, size, acc):
+        vals = []
         for k in range(subs):
             fac = jnp.exp2((mbuf[slot + k] - lse) * LOG2E) * scale
             ek = ebuf[pl.ds(base + k * size, size), :].reshape(size // 8, 8, toks)
-            dz = (ek * fac[None]).reshape(size, toks)
-            dz = jnp.where(iota[:size] == rel - (base + k * size), hot_val, dz)
-            dz_v[pl.ds(base + k * size, size), :] = dz.astype(BF16)
-        return acc + jnp.dot(et_s[:, pl.ds(base, subs * size)], dz_v[pl.ds(base, subs * size), :],
-                             preferred_element_type=F32)
+            dz = (ek * fac[None]).reshape(size // 16, 16, toks).astype(BF16)
+            here = (zero + (near - (base + k * size))).astype(jnp.int16)[None]
+            dz = jnp.where(iota16[:size // 16] == here, hot16, dz).reshape(size, toks)
+            dz_v[pl.ds(base + k * size, size), :] = dz
+            vals.append(dz)
+            if len(vals) * size == 256 or k == subs - 1:
+                done = (k + 1 - len(vals)) * size
+                acc = acc + jnp.dot(et_s[:, pl.ds(base + done, len(vals) * size)], jnp.concatenate(vals, axis=0),
+                                    preferred_element_type=F32)
+                vals = []
+        return acc
 
     def back_block(i, acc):
         return back(pl.multiple_of(i * blk, blk), i * per, per, SUB, acc)
 
-    dx_t = lax.fori_loop(0, nblk, back_block, jnp.zeros((dim, toks), F32))
+    dx_t = jnp.zeros((dim, toks), F32)
+    for i in range(nblk):
+        dx_t = back(i * blk, i * per, per, SUB, dx_t)
     if tail:
         dx_t = back(nblk * blk, nblk * per, 1, tail, dx_t)
     dx = dx_t.T
@@ -198,48 +214,24 @@
     for j in range(n):
         pk_tx[j, 0:local, :] = dx[j * local:(j + 1) * local]
         pk_tx[j, local:local + 8, :] = extra
-    parts = []
-    for d in range(1, n):
-        peer = lax.rem(me + d, n)
-        copy = pltpu.make_async_remote_copy(
-            src_ref=pk_tx.at[peer], dst_ref=pk_rx.at[me], send_sem=pk_send.at[d - 1], recv_sem=pk_recv.at[d - 1],
-            device_id={"tp": peer}, device_id_type=MESH)
-        copy.start()
-        parts.append(copy)
-    pk_rx[me] = pk_tx[me]
-    for copy in parts:
-        copy.wait_recv()
-
-    dx = sum(pk_rx[j, 0:local, :] for j in range(n))
-    extra = sum(pk_rx[j, local:local + 8, :] for j in range(n))
-    tgt_z = jnp.concatenate([extra[2 + c:3 + c] for c in range(toks // dim)], axis=1)
-    loss = (lse - tgt_z) * msk
-    mean_o[...] = jnp.sum(loss, axis=1, keepdims=True) / count
-    tok_o[...] = sum(jnp.where(me == j, loss[:, j * local:(j + 1) * local], 0.0) for j in range(n))
     own = pl.ds(pl.multiple_of(me * local, local), local)
-    xhat = xhat_s[own, :]
-    dxh = dx * ln_ref[0:1, :]
-    dh = rstd_s[own, :] * (dxh - jnp.mean(dxh, axis=-1, keepdims=True)
-                           - xhat * jnp.mean(dxh * xhat, axis=-1, keepdims=True))
-    dh_o[...] = dh.astype(BF16)
-    p_new, m_new, v_new = adam(ln_ref[...], extra[0:2], lm_ref[...], lv_ref[...], 0.0)
-    ln_o[...] = p_new
-    lmo[...] = m_new
-    lvo[...] = v_new
+    xh_o[...] = xhat_s[own, :]
+    rs_o[...] = rstd_s[own, :]
+    lse_o[...] = lse
+    msk_o[...] = msk
+    for d in range(n):
+        pks[d][...] = pk_tx[lax.rem(me + d, n)]
     m_copy.wait()
     v_copy.wait()
-    for copy in gathers + stats + parts:
+    for copy in gathers + stats:
         copy.wait_send()
 
 
 def update_kernel(e_v, m_v, v_v, dz_v, x_v, *rest):
-    small_in, big_out, small_out, (e_s, m_s, v_s, sem, small_sem) = rest[:6], rest[6:9], rest[9:15], rest[15:]
+    big_out, (e_s, m_s, v_s, sem) = rest[:3], rest[3:]
     rows, dim = e_v.shape
     nblk, per, tail = block_plan(rows)
     blk = per * SUB
-    smalls = [pltpu.make_async_copy(a, b, small_sem.at[k]) for k, (a, b) in enumerate(zip(small_in, small_out))]
-    for copy in smalls:
-        copy.start()
     stages = (e_s, m_s, v_s)
 
     def step(base, size):
@@ -261,8 +253,31 @@
         step(nblk * blk, tail)
     for k in range(3):
         pltpu.make_async_copy(stages[k], big_out[k], sem.at[k]).wait()
-    for copy in smalls:
-        copy.wait()
+
+
+def finish_kernel(n, xh_ref, rs_ref, lse_ref, msk_ref, ln_ref, lm_ref, lv_ref, *rest):
+    pks, (tok_o, mean_o, dh_o, ln_o, lmo, lvo, pk_rx) = rest[:n], rest[n:]
+    me = lax.axis_index("tp")
+    local, dim = xh_ref.shape
+    toks = n * local
+    for d in range(n):
+        pk_rx[lax.rem(me - d + n, n)] = pks[d][...]
+    dx = sum(pk_rx[j, 0:local, :] for j in range(n))
+    extra = sum(pk_rx[j, local:local + 8, :] for j in range(n))
+    tgt_z = jnp.concatenate([extra[2 + c:3 + c] for c in range(toks // dim)], axis=1)
+    msk = msk_ref[...]
+    loss = (lse_ref[...] - tgt_z) * msk
+    mean_o[...] = jnp.sum(loss, axis=1, keepdims=True) / jnp.sum(msk, axis=1, keepdims=True)
+    tok_o[...] = sum(jnp.where(me == j, loss[:, j * local:(j + 1) * local], 0.0) for j in range(n))
+    xhat = xh_ref[...]
+    dxh = dx * ln_ref[0:1, :]
+    dh = rs_ref[...] * (dxh - jnp.mean(dxh, axis=-1, keepdims=True)
+                        - xhat * jnp.mean(dxh * xhat, axis=-1, keepdims=True))
+    dh_o[...] = dh.astype(BF16)
+    p_new, m_new, v_new = adam(ln_ref[...], extra[0:2], lm_ref[...], lv_ref[...], 0.0)
+    ln_o[...] = p_new
+    lmo[...] = m_new
+    lvo[...] = v_new
 
 
 def solution(mesh):
@@ -283,45 +298,57 @@
         pad = -(-rows // 128) * 128
         big = [pltpu.VMEM((rows, dim), BF16), pltpu.VMEM((rows, dim), F32), pltpu.VMEM((rows, dim), F32),
                pltpu.VMEM((rows, toks), BF16), pltpu.VMEM((toks, dim), BF16)]
+        mid = [((local, dim), F32), ((local, dim), F32), ((1, toks), F32), ((1, toks), F32), ((2, dim), F32),
+               ((2, dim), F32), ((2, dim), F32)]
         small = [((1, local), F32), ((1, 1), F32), ((local, dim), BF16), ((2, dim), F32), ((2, dim), F32),
                  ((2, dim), F32)]
+        pack = [((local + 8, dim), F32)] * n
         dma = pltpu.SemaphoreType.DMA
+        hbm = lambda shape, dtype: jax.ShapeDtypeStruct(shape, dtype)
         mids = pl.pallas_call(
             functools.partial(forward_kernel, n),
             name="forward",
-            out_shape=big + [pltpu.VMEM(*s) for s in small],
+            out_shape=big + [pltpu.VMEM(*s) for s in mid] + [hbm(*s) for s in pack],
             in_specs=[anyw] * 9,
-            out_specs=[vmem] * 11,
+            out_specs=[vmem] * (12 + n),
             scratch_shapes=[
                 pltpu.VMEM((local, dim), BF16), pltpu.VMEM((1, local), jnp.int32), pltpu.VMEM((1, local), jnp.int32),
-                pltpu.VMEM((2, dim), F32), pltpu.VMEM((2, dim), F32), pltpu.VMEM((2, dim), F32),
                 pltpu.VMEM((n, local, dim), BF16), pltpu.VMEM((n, 1, local), jnp.int32),
                 pltpu.VMEM((n, 1, local), jnp.int32), pltpu.VMEM((toks, dim), F32), pltpu.VMEM((toks, dim), F32),
                 pltpu.VMEM((rows, toks), F32), pltpu.VMEM((nblk * per + 1, 8, toks), F32),
                 pltpu.VMEM((dim, pad), BF16),
                 pltpu.VMEM((2, toks), F32), pltpu.VMEM((n, 2, toks), F32),
-                pltpu.VMEM((n, local + 8, dim), F32), pltpu.VMEM((n, local + 8, dim), F32),
-                dma((9,)), dma((3, n - 1)), dma((3, n - 1)), dma((n - 1,)), dma((n - 1,)), dma((n - 1,)),
-                dma((n - 1,)),
+                pltpu.VMEM((n, local + 8, dim), F32),
+                dma((9,)), dma((3, n - 1)), dma((3, n - 1)), dma((n - 1,)), dma((n - 1,)),
             ],
             compiler_params=pltpu.CompilerParams(
                 collective_id=0, has_side_effects=True, vmem_limit_bytes=24 << 20),
         )(*[pltpu.with_memory_space_constraint(a, pltpu.HBM) for a in (
             hidden, targets.reshape(1, local), loss_mask.reshape(1, local), ln_params, ln_mom1, ln_mom2,
             out_embed, embed_mom1, embed_mom2)])
-        hbm = lambda shape, dtype: jax.ShapeDtypeStruct(shape, dtype)
-        outs = pl.pallas_call(
+        big_in, mid_in, packs = mids[:5], mids[5:12], mids[12:]
+        got = [packs[0]] + [
+            lax.ppermute(packs[d], "tp", [(i, (i + d) % n) for i in range(n)]) for d in range(1, n)]
+        e_new, m_new, v_new = pl.pallas_call(
             update_kernel,
             name="update",
-            out_shape=[hbm((rows, dim), BF16), hbm((rows, dim), F32), hbm((rows, dim), F32)]
-            + [hbm(*s) for s in small],
-            in_specs=[vmem] * 11,
-            out_specs=[anyw] * 9,
+            out_shape=[hbm((rows, dim), BF16), hbm((rows, dim), F32), hbm((rows, dim), F32)],
+            in_specs=[vmem] * 5,
+            out_specs=[anyw] * 3,
             scratch_shapes=[pltpu.VMEM((rows, dim), BF16), pltpu.VMEM((rows, dim), F32), pltpu.VMEM((rows, dim), F32),
-                            dma((3,)), dma((6,))],
+                            dma((3,))],
             compiler_params=pltpu.CompilerParams(vmem_limit_bytes=20 << 20),
-        )(*[pltpu.with_memory_space_constraint(a, pltpu.VMEM) for a in mids])
-        e_new, m_new, v_new, tok, mean, dh, ln_new, lm_new, lv_new = outs
+            cost_estimate=pl.CostEstimate(flops=50_000_000_000, bytes_accessed=32_000_000, transcendentals=0),
+        )(*[pltpu.with_memory_space_constraint(a, pltpu.VMEM) for a in big_in])
+        tok, mean, dh, ln_new, lm_new, lv_new = pl.pallas_call(
+            functools.partial(finish_kernel, n),
+            name="finish",
+            out_shape=[hbm(*s) for s in small],
+            in_specs=[vmem] * (7 + n),
+            out_specs=[vmem] * 6,
+            scratch_shapes=[pltpu.VMEM((n, local + 8, dim), F32)],
+            compiler_params=pltpu.CompilerParams(vmem_limit_bytes=4 << 20),
+        )(*mid_in, *got)
         return (tok.reshape(local), mean.reshape(1), dh, ln_new, lm_new, lv_new, e_new, m_new, v_new)
 
     return jax.shard_map(device_step, mesh=mesh, in_specs=(row_spec, tok_spec, tok_spec, repl_spec, vocab_spec, repl_spec, repl_spec, vocab_spec, vocab_spec), out_specs=(tok_spec, P("dp"), row_spec, part_spec, part_spec, part_spec, row_spec, row_spec, row_spec), check_vma=False)

time: 30.9 us -> 24.8 us (0.80)
  Pallas kernels: 30 us -> 21.7 us
  starting transfers between devices: 0 us -> 2.26 us
    pallas_call x1, Pallas kernels: 22.8 us -> 14.4 us  [device_step(): pl.pallas_call(functools.partial(forward_kernel, n), name='forward', out_...]
    ppermute x0 -> x3, starting transfers between devices: none -> 2.26 us  [device_step(): lax.ppermute(packs[d], 'tp', [(i, (i + d) % n) for i in range(n)])]
    pallas_call x0 -> x1, Pallas kernels: none -> 0.74 us  [device_step(): pl.pallas_call(functools.partial(finish_kernel, n), name='finish', out_sh...]
    pallas_call x1, Pallas kernels: 7.21 us -> 6.54 us  [device_step(): pl.pallas_call(update_kernel, name='update', out_shape=[hbm((rows, dim),...]
  transfers between devices with their start and end apart: 0 -> 3, of which waited for: 0 -> 0; matrix products, arithmetic and copies ran while one was open for 0% -> 0% of each run, Pallas kernels for 0% -> 27%
where the time goes in v3:
time: 24.8 us; the launch traced here: 24.6 us
  Pallas kernels  21.7 us (88%)
  starting transfers between devices  2.26 us (9%)
  between operations  0.69 us (3%)
    pallas_call x1, Pallas kernels, device_step(): pl.pallas_call(functools.partial(forward_kernel, n), name='forward', out_...  14.4 us
    pallas_call x1, Pallas kernels, device_step(): pl.pallas_call(update_kernel, name='update', out_shape=[hbm((rows, dim),...  6.54 us
    ppermute x3, starting transfers between devices, device_step(): lax.ppermute(packs[d], 'tp', [(i, (i + d) % n) for i in range(n)])  2.26 us
    pallas_call x1, Pallas kernels, device_step(): pl.pallas_call(functools.partial(finish_kernel, n), name='finish', out_sh...  0.74 us
  transfers between devices with their start and end apart: 3, of which 0 were waited for; matrix products, arithmetic and copies ran while one was open for 0% of the time, Pallas kernels for 27%

profile of v3, /device:TPU:0, one launch (start us, length us, event | category | flops | bytes accessed | tf_op | source)
XLA Modules:
  0.0 24.6 jit_solution(5991990064588685493)
XLA Ops:
  0.6 14.4 %forward.1 = (bf16[12576,128]{1,0:T(8,128)(2,1)S(1)}, f32[12576,128]{1,0:T(8,128)S(1)}, f32[12576,128]{1,0:T(8,128)S(1)}, bf16[12576,256]{1,0:T(8,128)(2,1)S(1)}...) custom-call(bf16[64,128]{1,0:T(8,128)(2,1)} %hid_hbm.1, ...), custom_call_target="tpu_custom_call" | custom-call | tf_op jit(solution)/shard_map/forward/pallas_call | solution.py:308
  15.0 0.1 collective-permute-start
  15.2 0.8 %collective-permute-start.1 = (f32[72,128]{1,0:T(8,128)S(1)}, f32[72,128]{1,0:T(8,128)S(1)}, u32[]{:S(2)}, u32[]{:S(2)}) collective-permute-start(f32[72,128]{1,0:T(8,128)S(1)} %get-tuple-element.43), channel_id=1, source_target_pairs={{0,2},{1,3},{2,0},{3,1},{4,6},{5,7},{6,4},{7,5}} | collective-permute-start | bytes 110600 | tf_op jit(solution)/shard_map/ppermute | solution.py:331
  16.0 1.4 %collective-permute-start.2 = (f32[72,128]{1,0:T(8,128)S(1)}, f32[72,128]{1,0:T(8,128)S(1)}, u32[]{:S(2)}, u32[]{:S(2)}) collective-permute-start(f32[72,128]{1,0:T(8,128)S(1)} %get-tuple-element.44), channel_id=1, source_target_pairs={{0,3},{1,0},{2,1},{3,2},{4,7},{5,4},{6,5},{7,6}} | collective-permute-start | bytes 110600 | tf_op jit(solution)/shard_map/ppermute | solution.py:331
  17.3 6.5 %update.1 = (bf16[12576,128]{1,0:T(8,128)(2,1)}, f32[12576,128]{1,0:T(8,128)}, f32[12576,128]{1,0:T(8,128)}) custom-call(bf16[12576,128]{1,0:T(8,128)(2,1)S(1)} %get-tuple-element.51.e_v, f32[12576,128]{1,0:T(8,128)S(1)} %get-tuple-element.52.m_v, f32[12576,128]{1,0:T(8,128)S(1)} %get-tuple-element.53.v_v, bf16[12576,256]{1,0:T(8,128)(2,1)S(1)} %get-tuple-element.54.dz_v, ...), custom_call_target="tpu_custom_call" | custom-call | flops 49999998976 | bytes 32000000 | tf_op jit(solution)/shard_map/update/pallas_call | solution.py:332
  23.9 0.0 collective-permute-done.rest_1_
  23.9 0.0 collective-permute-done.1.rest_2_
  23.9 0.0 collective-permute-done.2.rest_3_
  23.9 0.7 %finish.1 = (f32[1,64]{1,0:T(1,128)}, f32[1,1]{1,0:T(1,128)}, bf16[64,128]{1,0:T(8,128)(2,1)}, f32[2,128]{1,0:T(2,128)}, f32[2,128]{1,0:T(2,128)}, /*index=5*/f32[2,128]{1,0:T(2,128)}) custom-call(f32[64,128]{1,0:T(8,128)S(1)} %get-tuple-element.34.xh_ref, f32[64,128]{1,0:T(8,128)S(1)} %get-tuple-element.35.rs_ref, f32[1,256]{1,0:T(1,128)S(1)} %get-tuple-element.36.lse_ref, ...), custom_call_target="tpu_custom_call" | custom-call | tf_op jit(solution)/shard_map/finish/pallas_call | solution.py:343
Async XLA Ops:
  15.0 8.8 %collective-permute-start = (f32[72,128]{1,0:T(8,128)S(1)}, f32[72,128]{1,0:T(8,128)S(1)}, u32[]{:S(2)}, u32[]{:S(2)}) collective-permute-start(f32[72,128]{1,0:T(8,128)S(1)} %get-tuple-element.42), channel_id=1, source_target_pairs={{0,1},{1,2},{2,3},{3,0},{4,5},{5,6},{6,7},{7,4}} | collective-permute-start | bytes 110600 | tf_op jit(solution)/shard_map/ppermute | solution.py:331
  15.2 8.7 %collective-permute-start.1 = (f32[72,128]{1,0:T(8,128)S(1)}, f32[72,128]{1,0:T(8,128)S(1)}, u32[]{:S(2)}, u32[]{:S(2)}) collective-permute-start(f32[72,128]{1,0:T(8,128)S(1)} %get-tuple-element.43), channel_id=1, source_target_pairs={{0,2},{1,3},{2,0},{3,1},{4,6},{5,7},{6,4},{7,5}} | collective-permute-start | bytes 110600 | tf_op jit(solution)/shard_map/ppermute | solution.py:331
  16.0 7.9 %collective-permute-start.2 = (f32[72,128]{1,0:T(8,128)S(1)}, f32[72,128]{1,0:T(8,128)S(1)}, u32[]{:S(2)}, u32[]{:S(2)}) collective-permute-start(f32[72,128]{1,0:T(8,128)S(1)} %get-tuple-element.44), channel_id=1, source_target_pairs={{0,3},{1,0},{2,1},{3,2},{4,7},{5,4},{6,5},{7,6}} | collective-permute-start | bytes 110600 | tf_op jit(solution)/shard_map/ppermute | solution.py:331

commit v4 on v0

v4 whole, which is shorter than its diff:
```python
import functools

import jax
import jax.numpy as jnp
from jax import lax
from jax.experimental import pallas as pl
from jax.experimental.pallas import tpu as pltpu
from jax.sharding import PartitionSpec as P

LN_EPS = 1e-5
BETA_ONE = 0.9
BETA_TWO = 0.95
ADAM_EPS = 1e-8
LEARN_RATE = 1e-3
WEIGHT_DECAY = 0.1
ADAM_STEP = 10
LOG2E = 1.4426950408889634
TINY = 1e-37
SUB = 128
CHUNK = 896
EARLY = 2
DOT = 896
MESH = pl.DeviceIdType.MESH
F32 = jnp.float32
BF16 = jnp.bfloat16


def pair_plan(rows):
    half = rows // 2
    return half, half // SUB, half % SUB


def row_blocks(rows):
    full = rows // CHUNK
    return [(i * CHUNK, CHUNK) for i in range(full)] + ([(full * CHUNK, rows - full * CHUNK)] if rows % CHUNK else [])


def adam_const():
    one = 1.0 - BETA_ONE ** ADAM_STEP
    two = 1.0 - BETA_TWO ** ADAM_STEP
    root = two ** 0.5
    return LEARN_RATE * root / one, ADAM_EPS * root


def adam(param, grad, m_old, v_old, decay):
    scale, eps = adam_const()
    m_new = BETA_ONE * m_old + (1.0 - BETA_ONE) * grad
    v_new = BETA_TWO * v_old + ((1.0 - BETA_TWO) * grad) * grad
    root = v_new * lax.rsqrt(v_new + TINY)
    kept = param if decay == 0.0 else (1.0 - LEARN_RATE * decay) * param
    return kept - (scale * m_new) / (root + eps), m_new, v_new


def adam_rows(base, size, e_in, m_in, v_in, dz_v, x_v, e_out, m_out, v_out, shift):
    sl, to = pl.ds(base, size), pl.ds(base - shift, size)
    g = jnp.dot(dz_v[sl, :], x_v[...], preferred_element_type=F32)
    p_new, m_new, v_new = adam(e_in[sl, :].astype(F32), g, m_in[sl, :], v_in[sl, :], WEIGHT_DECAY)
    e_out[to, :] = p_new.astype(BF16)
    m_out[to, :] = m_new
    v_out[to, :] = v_new


def place():
    me = lax.axis_index("tp")
    side, core = me // 2, lax.rem(me, 2)
    far = 2 - 2 * side
    return me, core, (me + 1 - 2 * core, far + core, far + 1 - core)


def swap(v):
    half = v.shape[1] // 2
    return jnp.concatenate([v[:, half:], v[:, :half]], axis=1)


def forward_kernel(n, hid_hbm, tgt_hbm, msk_hbm, ln_hbm, lm_hbm, lv_hbm, e_hbm, m_hbm, v_hbm,
                   e_v, m_v, v_v, dz_v, x_v, keep_o, away_o, xh_o, rs_o, lse_o, msk_o, ln_ref, lm_ref, lv_ref,
                   hid_ref, tgt_ref, msk_ref, hid_s, tgt_s, msk_s, xhat_s, rstd_s, dx_s, xd_s, ebuf, mbuf, et_s,
                   st_tx, st_rx, pk_tx, pk_rx,
                   load_sem, in_send, in_recv, st_send, st_recv, pk_send, pk_recv):
    me, core, peers = place()
    rows, dim = e_v.shape
    local = hid_ref.shape[0]
    toks = n * local
    wide = toks // 2
    half, subs, tail = pair_plan(rows)
    units = [((i // subs) * half + (i % subs) * SUB, i * SUB, SUB) for i in range(2 * subs)]

    barrier = pltpu.get_barrier_semaphore()
    for peer in peers:
        pl.semaphore_signal(barrier, inc=1, device_id={"tp": peer}, device_id_type=MESH)
    firsts = [pltpu.make_async_copy(a, b, load_sem.at[3 + k]) for k, (a, b) in enumerate((
        (hid_hbm, hid_ref), (tgt_hbm, tgt_ref), (msk_hbm, msk_ref), (ln_hbm, ln_ref), (lm_hbm, lm_ref),
        (lv_hbm, lv_ref)))]
    for copy in firsts:
        copy.start()
    e_copy = pltpu.make_async_copy(e_hbm, e_v, load_sem.at[0])
    m_copy = pltpu.make_async_copy(m_hbm, m_v, load_sem.at[1])
    v_copy = pltpu.make_async_copy(v_hbm, v_v, load_sem.at[2])
    e_copy.start()
    for copy in firsts:
        copy.wait()
    pl.semaphore_wait(barrier, n - 1)

    def send(src, dst, peer, send_sem, recv_sem):
        copy = pltpu.make_async_remote_copy(src_ref=src, dst_ref=dst, send_sem=send_sem, recv_sem=recv_sem,
                                            device_id={"tp": peer}, device_id_type=MESH)
        copy.start()
        return copy

    gathers = []
    for k, (src, dst) in enumerate(((hid_ref, hid_s), (tgt_ref, tgt_s), (msk_ref, msk_s))):
        dst[core] = src[...]
        for r, peer in enumerate(peers):
            gathers.append(send(src, dst.at[2 + core if r else core], peer, in_send.at[k, r], in_recv.at[k, r]))
    xd_s[...] = jnp.zeros(xd_s.shape, BF16)
    e_copy.wait()
    m_copy.start()
    v_copy.start()

    def norm(h):
        lanes = slice(h * wide, (h + 1) * wide)
        hid = hid_s[2 * h:2 * h + 2].reshape(wide, dim).astype(F32)
        cent = hid - jnp.mean(hid, axis=-1, keepdims=True)
        rstd = lax.rsqrt(jnp.mean(cent * cent, axis=-1, keepdims=True) + LN_EPS)
        xhat = cent * rstd
        x_b = (xhat * ln_ref[0:1, :] + ln_ref[1:2, :]).astype(BF16)
        x_v[lanes, :] = x_b
        x_t = x_b.T
        xd_s[h, 0:dim, 0:wide] = x_t
        xd_s[h, dim:2 * dim, wide:2 * wide] = x_t
        xhat_s[lanes, :] = xhat
        rstd_s[lanes, :] = jnp.broadcast_to(rstd, (wide, dim))

    def forward(h):
        top = jnp.full((8, toks), -jnp.inf, F32)
        total = jnp.zeros((8, toks), F32)
        for first in range(0, half, DOT):
            span = min(DOT, half - first)
            pair = jnp.concatenate([e_v[pl.ds(first, span), :], e_v[pl.ds(half + first, span), :]], axis=1)
            z = jnp.dot(pair, xd_s[h], preferred_element_type=F32)
            for k in range(0, span, SUB):
                size = min(SUB, span - k)
                zk = z[k:k + size].reshape(size // 8, 8, toks)
                new = jnp.maximum(top, jnp.max(zk, axis=0))
                ek = jnp.exp2((zk - new[None]) * LOG2E)
                ebuf[h, pl.ds(first + k, size), :] = ek.reshape(size, toks)
                mbuf[h, (first + k) // SUB] = new
                total = total * jnp.exp2((top - new) * LOG2E) + jnp.sum(ek, axis=0)
                top = new
        peak = jnp.max(top, axis=0, keepdims=True)
        peak = jnp.maximum(peak[:, :wide], peak[:, wide:])
        peak2 = jnp.concatenate([peak, peak], axis=1)
        total = jnp.sum(total * jnp.exp2((top - peak2) * LOG2E), axis=0, keepdims=True)
        st_tx[0:1, h * wide:(h + 1) * wide] = peak
        st_tx[1:2, h * wide:(h + 1) * wide] = total[:, :wide] + total[:, wide:]

    gathers[0].wait_recv()
    norm(0)
    forward(0)
    for copy in gathers[1:]:
        copy.wait_recv()
    norm(1)
    forward(1)
    stats = [send(st_tx, st_rx.at[r], peer, st_send.at[r], st_recv.at[r]) for r, peer in enumerate(peers)]

    tgt = jnp.concatenate([tgt_s[j] for j in range(n)], axis=1)
    msk = jnp.concatenate([msk_s[j] for j in range(n)], axis=1).astype(F32)
    count = jnp.sum(msk, axis=1, keepdims=True)
    scale = msk / count
    rel = tgt - me * rows
    inside = (rel >= 0) & (rel < rows)
    near = jnp.where(inside, rel, -15000)
    for low, col, size in units:
        et_s[:, pl.ds(col, size)] = e_v[pl.ds(low, size), :].T
    ends = [h * half + subs * SUB for h in range(2)]
    if tail:
        et_s[:, pl.ds(2 * subs * SUB, 2 * tail)] = jnp.concatenate([e_v[pl.ds(low, tail), :] for low in ends], axis=0).T

    flat = jnp.zeros((16, toks), jnp.int32)
    iota16 = lax.broadcasted_iota(jnp.int32, (SUB, toks), 0).astype(jnp.int16).reshape(SUB // 16, 16, toks)

    def hit(low, size):
        return iota16[:size // 16] == (flat + (near - low)).astype(jnp.int16)[None]

    def gather_sum(value):
        accs = [jnp.zeros((dim, toks), F32)] * 2
        groups = [units[i:i + 2] for i in range(0, len(units), 2)]
        if tail:
            groups.append([(low, 2 * subs * SUB + h * tail, tail) for h, low in enumerate(ends)])
        for i, group in enumerate(groups):
            vals = jnp.concatenate([value(low, size) for low, _, size in group], axis=0)
            accs[i % 2] = accs[i % 2] + jnp.dot(et_s[:, pl.ds(group[0][1], vals.shape[0])], vals,
                                                preferred_element_type=F32)
        return accs[0] - accs[1] * -1.0

    ones, none = jnp.ones((1, 16, toks), BF16), jnp.zeros((1, 16, toks), BF16)
    rows_t = gather_sum(lambda low, size: jnp.where(hit(low, size), ones, none).reshape(size, toks))
    tgt_z = jnp.sum(x_v[...].astype(F32).T * rows_t, axis=0, keepdims=True)
    tgt_z = jnp.where(inside, tgt_z, 0.0)

    for copy in stats:
        copy.wait_recv()
    both = [st_tx[...], st_rx[0], swap(st_rx[1]), swap(st_rx[2])]
    peak = jnp.maximum(jnp.maximum(both[0][0:1], both[1][0:1]), jnp.maximum(both[2][0:1], both[3][0:1]))
    sums = [v[1:2] * jnp.exp2((v[0:1] - peak) * LOG2E) for v in both]
    lse = peak + jnp.log((sums[0] + sums[1]) + (sums[2] + sums[3]))
    hot_val = (jnp.exp2((tgt_z - lse) * LOG2E) - 1.0) * scale
    hot16 = jnp.broadcast_to(hot_val, (16, toks)).astype(BF16)[None]

    def grads(low, size):
        h, first = low // half, low % half
        sides = slice(h * wide, (h + 1) * wide)
        seen = jnp.concatenate([mbuf[c, first // SUB, :, sides] for c in range(2)], axis=1)
        fac = jnp.exp2((seen - lse) * LOG2E) * scale
        ek = jnp.concatenate([ebuf[c, pl.ds(first, size), sides] for c in range(2)], axis=1)
        dz = (ek.reshape(size // 8, 8, toks) * fac[None]).reshape(size // 16, 16, toks).astype(BF16)
        dz = jnp.where(hit(low, size), hot16, dz).reshape(size, toks)
        dz_v[pl.ds(low, size), :] = dz
        return dz

    dx = gather_sum(grads).T
    extra = jnp.concatenate(
        [jnp.sum(dx * xhat_s[...], axis=0, keepdims=True), jnp.sum(dx, axis=0, keepdims=True)]
        + [tgt_z[:, c * dim:(c + 1) * dim] for c in range(toks // dim)]
        + [jnp.zeros((6 - toks // dim, dim), F32)], axis=0)
    dx_s[...] = dx
    for c in range(2):
        pk_tx[c, 0:local, :] = dx_s[pl.ds(pl.multiple_of(c * wide + (1 - core) * local, local), local), :]
        pk_tx[c, local:local + 8, :] = extra
    part = send(pk_tx, pk_rx, peers[0], pk_send, pk_recv)

    own = pl.ds(pl.multiple_of(core * local, local), local)
    xh_o[...] = xhat_s[own, :]
    rs_o[...] = rstd_s[own, :]
    msk_o[...] = msk
    lse_o[...] = lse
    m_copy.wait()
    v_copy.wait()
    for base, size in row_blocks(rows)[:EARLY]:
        adam_rows(base, size, e_v, m_v, v_v, dz_v, x_v, e_v, m_v, v_v, 0)

    part.wait_recv()
    for c, out in enumerate((keep_o, away_o)):
        mine = pl.ds(pl.multiple_of(c * wide + core * local, local), local)
        out[0:local, :] = dx_s[mine, :] + pk_rx[c, 0:local, :]
        out[local:local + 8, :] = extra + pk_rx[c, local:local + 8, :]
    for copy in gathers + stats + [part]:
        copy.wait_send()


def update_kernel(e_v, m_v, v_v, dz_v, x_v, e_o, m_o, v_o, e_s, m_s, v_s, sem):
    rows = e_v.shape[0]
    blocks = row_blocks(rows)
    shift = blocks[EARLY][0]
    outs = (e_o, m_o, v_o)
    copies = []
    for b, (base, size) in enumerate(blocks[:EARLY]):
        for k, src in enumerate((e_v, m_v, v_v)):
            copy = pltpu.make_async_copy(src.at[pl.ds(base, size)], outs[k].at[pl.ds(base, size)], sem.at[k, b])
            copy.start()
            copies.append(copy)
    for b, (base, size) in enumerate(blocks[EARLY:]):
        adam_rows(base, size, e_v, m_v, v_v, dz_v, x_v, e_s, m_s, v_s, shift)
        for k, src in enumerate((e_s, m_s, v_s)):
            copy = pltpu.make_async_copy(src.at[pl.ds(base - shift, size)], outs[k].at[pl.ds(base, size)],
                                         sem.at[k, EARLY + b])
            copy.start()
            copies.append(copy)

    for copy in copies:
        copy.wait()


def finish_kernel(n, keep_ref, xh_ref, rs_ref, lse_ref, msk_ref, ln_ref, lm_ref, lv_ref, got_ref,
                  tok_o, mean_o, dh_o, ln_o, lmo, lvo):
    _, core, _ = place()
    local, dim = xh_ref.shape
    wide = n * local // 2
    keep, got = keep_ref[...], got_ref[...]
    both = keep + got
    dx, extra = both[0:local], both[local:local + 8]
    near, far = keep[local + 2:local + 4], got[local + 2:local + 4]
    tgt_z = jnp.concatenate([near[0:1] + far[1:2], near[1:2] + far[0:1]], axis=1)
    msk = msk_ref[...]
    loss = (lse_ref[...] - tgt_z) * msk
    mean_o[...] = jnp.sum(loss[:, :wide] + loss[:, wide:], axis=1, keepdims=True) / jnp.sum(msk, axis=1, keepdims=True)
    tok_o[...] = jnp.where(core == 0, loss[:, :local], loss[:, local:wide])
    xhat = xh_ref[...]
    dxh = dx * ln_ref[0:1, :]
    dh = rs_ref[...] * (dxh - jnp.mean(dxh, axis=-1, keepdims=True)
                        - xhat * jnp.mean(dxh * xhat, axis=-1, keepdims=True))
    dh_o[...] = dh.astype(BF16)
    p_new, m_new, v_new = adam(ln_ref[...], extra[0:2], lm_ref[...], lv_ref[...], 0.0)
    ln_o[...] = p_new
    lmo[...] = m_new
    lvo[...] = v_new


def solution(mesh):
    n = mesh.shape["tp"]
    row_spec = P(("dp", "tp"), None)
    tok_spec = P(("dp", "tp"))
    vocab_spec = P("tp", None)
    repl_spec = P()
    part_spec = P("dp", None)
    vmem = pl.BlockSpec(memory_space=pltpu.VMEM)
    hbm = pl.BlockSpec(memory_space=pltpu.HBM)

    def device_step(hidden, targets, loss_mask, ln_params, out_embed, ln_mom1, ln_mom2, embed_mom1, embed_mom2):
        local, dim = hidden.shape
        rows = out_embed.shape[0]
        toks = n * local
        half = rows // 2
        blocks = row_blocks(rows)
        late = rows - blocks[EARLY][0]
        big = [((rows, dim), BF16), ((rows, dim), F32), ((rows, dim), F32)]
        pack = ((local + 8, dim), F32)
        mid = big + [((rows, toks), BF16), ((toks, dim), BF16), pack, pack, ((local, dim), F32), ((local, dim), F32),
                     ((1, toks), F32), ((1, toks), F32), ((2, dim), F32), ((2, dim), F32), ((2, dim), F32)]
        small = [((1, local), F32), ((1, 1), F32), ((local, dim), BF16), ((2, dim), F32), ((2, dim), F32),
                 ((2, dim), F32)]
        dma = pltpu.SemaphoreType.DMA
        peers = n - 1
        mids = pl.pallas_call(
            functools.partial(forward_kernel, n),
            name="forward",
            out_shape=[pltpu.VMEM(*s) for s in mid],
            in_specs=[hbm] * 9,
            out_specs=[vmem] * len(mid),
            scratch_shapes=[
                pltpu.VMEM((local, dim), BF16), pltpu.VMEM((1, local), jnp.int32), pltpu.VMEM((1, local), jnp.int32),
                pltpu.VMEM((n, local, dim), BF16), pltpu.VMEM((n, 1, local), jnp.int32),
                pltpu.VMEM((n, 1, local), jnp.int32), pltpu.VMEM((toks, dim), F32), pltpu.VMEM((toks, dim), F32),
                pltpu.VMEM((toks, dim), F32),
                pltpu.VMEM((2, 2 * dim, toks), BF16), pltpu.VMEM((2, half, toks), F32),
                pltpu.VMEM((2, -(-half // SUB), 8, toks), F32), pltpu.VMEM((dim, -(-rows // 128) * 128), BF16),
                pltpu.VMEM((2, toks), F32), pltpu.VMEM((peers, 2, toks), F32),
                pltpu.VMEM((n // 2, local + 8, dim), F32), pltpu.VMEM((n // 2, local + 8, dim), F32),
                dma((9,)), dma((3, peers)), dma((3, peers)), dma((peers,)), dma((peers,)), dma, dma,
            ],
            compiler_params=pltpu.CompilerParams(
                collective_id=0, has_side_effects=True, vmem_limit_bytes=26 << 20),
        )(*[pltpu.with_memory_space_constraint(a, pltpu.HBM) for a in (
            hidden, targets.reshape(1, local), loss_mask.reshape(1, local), ln_params, ln_mom1, ln_mom2,
            out_embed, embed_mom1, embed_mom2)])
        got = lax.ppermute(mids[6], "tp", [(i, (i + n // 2) % n) for i in range(n)])
        e_new, m_new, v_new = pl.pallas_call(
            update_kernel,
            name="update",
            out_shape=[jax.ShapeDtypeStruct(*s) for s in big],
            in_specs=[vmem] * 5,
            out_specs=[hbm] * 3,
            scratch_shapes=[
                pltpu.VMEM((late, dim), BF16), pltpu.VMEM((late, dim), F32), pltpu.VMEM((late, dim), F32),
                dma((3, len(blocks)))],
            compiler_params=pltpu.CompilerParams(vmem_limit_bytes=20 << 20),
            cost_estimate=pl.CostEstimate(flops=50_000_000_000, bytes_accessed=32_000_000, transcendentals=0),
        )(*[pltpu.with_memory_space_constraint(a, pltpu.VMEM) for a in mids[:5]])
        tok, mean, dh, ln_new, lm_new, lv_new = pl.pallas_call(
            functools.partial(finish_kernel, n),
            name="finish",
            out_shape=[jax.ShapeDtypeStruct(*s) for s in small],
            in_specs=[vmem] * 9,
            out_specs=[vmem] * 6,
            compiler_params=pltpu.CompilerParams(vmem_limit_bytes=4 << 20),
        )(mids[5], *mids[7:], got)
        return (tok.reshape(local), mean.reshape(1), dh, ln_new, lm_new, lv_new, e_new, m_new, v_new)

    return jax.shard_map(device_step, mesh=mesh, in_specs=(row_spec, tok_spec, tok_spec, repl_spec, vocab_spec, repl_spec, repl_spec, vocab_spec, vocab_spec), out_specs=(tok_spec, P("dp"), row_spec, part_spec, part_spec, part_spec, row_spec, row_spec, row_spec), check_vma=False)
```

time: 109 us -> 22.4 us (0.21)
  blocking collectives: 32.2 us -> 0 us
  other arithmetic: 27.4 us -> 0 us
  matrix products: 24.4 us -> 0 us
  Pallas kernels: 0 us -> 20.7 us
  between operations: 17.3 us -> 0.67 us
  local copies, waits for them, and re-layouts: 7.04 us -> 0 us
    dot_general x3 -> x0, matrix products: 24.4 us -> none  [the longest x1 12.9 us: device_step(): lax.dot_general(d_logits, x_full, (((0,), (0,)), ((), ())), preferred_ele...]
    pallas_call x0 -> x3, Pallas kernels: none -> 20.7 us  [the longest x1 14 us: device_step(): pl.pallas_call(functools.partial(forward_kernel, n), name='forward', out_...]
    reduce_sum x7 -> x0, other arithmetic: 15.6 us -> none  [the longest x1 10.1 us: device_step(): local_sum = jnp.sum(jnp.exp(logits - local_max[:, None]), axis=1)]
    psum x2 -> x0, blocking collectives: 12.2 us -> none  [the longest x1 6.56 us: device_step(): lax.psum(jnp.stack([local_sum * jnp.exp(local_max - global_max), tgt_logi...]
    convert_element_type x3 -> x0, other arithmetic: 11.2 us -> none  [the longest x1 9.68 us: device_step(): ((jnp.exp(logits - log_norm[:, None]) - is_target.astype(jnp.float32)) *...]
    all_gather x1 -> x0, blocking collectives: 7.56 us -> none  [device_step(): x_full = lax.all_gather(x_norm.astype(jnp.bfloat16), 'tp', tiled=True)]
    unnamed x1 -> x0, blocking collectives: 6.75 us -> none
    unnamed x17 -> x0, local copies, waits for them, and re-layouts: 5.68 us -> none
  transfers between devices with their start and end apart: 1 -> 1, of which waited for: 0 -> 0; matrix products, arithmetic and copies ran while one was open for 12% -> 0% of each run, Pallas kernels for 0% -> 27%
where the time goes in v4:
time: 22.4 us; the launch traced here: 22.2 us
  Pallas kernels  20.7 us (92%)
  starting transfers between devices  0.79 us (4%)
  between operations  0.67 us (3%)
    pallas_call x1, Pallas kernels, device_step(): pl.pallas_call(functools.partial(forward_kernel, n), name='forward', out_...  14 us
    pallas_call x1, Pallas kernels, device_step(): pl.pallas_call(update_kernel, name='update', out_shape=[jax.ShapeDtypeStr...  6.01 us
    ppermute x1, starting transfers between devices, device_step(): got = lax.ppermute(mids[6], 'tp', [(i, (i + n // 2) % n) for i in range(n)])  0.79 us
    pallas_call x1, Pallas kernels, device_step(): pl.pallas_call(functools.partial(finish_kernel, n), name='finish', out_sh...  0.72 us
  transfers between devices with their start and end apart: 1, of which 0 were waited for; matrix products, arithmetic and copies ran while one was open for 0% of the time, Pallas kernels for 27%

profile of v4, /device:TPU:0, one launch (start us, length us, event | category | flops | bytes accessed | tf_op | source)
XLA Modules:
  0.0 22.2 jit_solution(3482057296110327767)
XLA Ops:
  0.6 14.0 %forward.1 = (bf16[12576,128]{1,0:T(8,128)(2,1)S(1)}, f32[12576,128]{1,0:T(8,128)S(1)}, f32[12576,128]{1,0:T(8,128)S(1)}, bf16[12576,256]{1,0:T(8,128)(2,1)S(1)}...) custom-call(bf16[64,128]{1,0:T(8,128)(2,1)} %hid_hbm.1, ...), custom_call_target="tpu_custom_call" | custom-call | tf_op jit(solution)/shard_map/forward/pallas_call | solution.py:324
  14.6 0.8 %collective-permute-start = (f32[72,128]{1,0:T(8,128)S(1)}, f32[72,128]{1,0:T(8,128)S(1)}, u32[]{:S(2)}, u32[]{:S(2)}) collective-permute-start(f32[72,128]{1,0:T(8,128)S(1)} %get-tuple-element.40), channel_id=1, source_target_pairs={{0,2},{1,3},{2,0},{3,1},{4,6},{5,7},{6,4},{7,5}} | collective-permute-start | bytes 110600 | tf_op jit(solution)/shard_map/ppermute | solution.py:346
  15.4 6.0 %update.1 = (bf16[12576,128]{1,0:T(8,128)(2,1)}, f32[12576,128]{1,0:T(8,128)}, f32[12576,128]{1,0:T(8,128)}) custom-call(bf16[12576,128]{1,0:T(8,128)(2,1)S(1)} %get-tuple-element.47.e_v, f32[12576,128]{1,0:T(8,128)S(1)} %get-tuple-element.48.m_v, f32[12576,128]{1,0:T(8,128)S(1)} %get-tuple-element.49.v_v, bf16[12576,256]{1,0:T(8,128)(2,1)S(1)} %get-tuple-element.50.dz_v, ...), custom_call_target="tpu_custom_call" | custom-call | flops 49999998976 | bytes 32000000 | tf_op jit(solution)/shard_map/update/pallas_call | solution.py:347
  21.4 0.0 collective-permute-done.got_ref
  21.5 0.7 %finish.1 = (f32[1,64]{1,0:T(1,128)}, f32[1,1]{1,0:T(1,128)}, bf16[64,128]{1,0:T(8,128)(2,1)}, f32[2,128]{1,0:T(2,128)}, f32[2,128]{1,0:T(2,128)}, /*index=5*/f32[2,128]{1,0:T(2,128)}) custom-call(f32[72,128]{1,0:T(8,128)S(1)} %get-tuple-element.32.keep_ref, f32[64,128]{1,0:T(8,128)S(1)} %get-tuple-element.33.xh_ref, ...), custom_call_target="tpu_custom_call" | custom-call | tf_op jit(solution)/shard_map/finish/pallas_call | solution.py:359
Async XLA Ops:
  14.6 6.8 %collective-permute-start = (f32[72,128]{1,0:T(8,128)S(1)}, f32[72,128]{1,0:T(8,128)S(1)}, u32[]{:S(2)}, u32[]{:S(2)}) collective-permute-start(f32[72,128]{1,0:T(8,128)S(1)} %get-tuple-element.40), channel_id=1, source_target_pairs={{0,2},{1,3},{2,0},{3,1},{4,6},{5,7},{6,4},{7,5}} | collective-permute-start | bytes 110600 | tf_op jit(solution)/shard_map/ppermute | solution.py:346

commit v5 on v4

--- a/solution.py
+++ b/solution.py
@@ -17,8 +17,8 @@
 LOG2E = 1.4426950408889634
 TINY = 1e-37
 SUB = 128
-CHUNK = 896
-EARLY = 2
+CHUNK = 448
+EARLY = 4
 DOT = 896
 MESH = pl.DeviceIdType.MESH
 F32 = jnp.float32
@@ -73,13 +73,12 @@
 
 
 def forward_kernel(n, hid_hbm, tgt_hbm, msk_hbm, ln_hbm, lm_hbm, lv_hbm, e_hbm, m_hbm, v_hbm,
-                   e_v, m_v, v_v, dz_v, x_v, keep_o, away_o, xh_o, rs_o, lse_o, msk_o, ln_ref, lm_ref, lv_ref,
-                   hid_ref, tgt_ref, msk_ref, hid_s, tgt_s, msk_s, xhat_s, rstd_s, dx_s, xd_s, ebuf, mbuf, et_s,
-                   st_tx, st_rx, pk_tx, pk_rx,
-                   load_sem, in_send, in_recv, st_send, st_recv, pk_send, pk_recv):
+                   e_v, m_v, v_v, dz_v, x_v, keep_o, away_o, xh_o, rs_o, lse_o, msk_o, lns_o,
+                   hid_s, ids_s, xhat_s, rstd_s, dx_s, xd_s, ebuf, mbuf, et_s, st_tx, st_rx, pk_tx, pk_rx,
+                   load_sem, hid_send, near_recv, far_recv, ids_send, ids_recv, st_send, st_recv, pk_send, pk_recv):
     me, core, peers = place()
     rows, dim = e_v.shape
-    local = hid_ref.shape[0]
+    local = hid_hbm.shape[0]
     toks = n * local
     wide = toks // 2
     half, subs, tail = pair_plan(rows)
@@ -88,17 +87,15 @@
     barrier = pltpu.get_barrier_semaphore()
     for peer in peers:
         pl.semaphore_signal(barrier, inc=1, device_id={"tp": peer}, device_id_type=MESH)
-    firsts = [pltpu.make_async_copy(a, b, load_sem.at[3 + k]) for k, (a, b) in enumerate((
-        (hid_hbm, hid_ref), (tgt_hbm, tgt_ref), (msk_hbm, msk_ref), (ln_hbm, ln_ref), (lm_hbm, lm_ref),
-        (lv_hbm, lv_ref)))]
-    for copy in firsts:
-        copy.start()
     e_copy = pltpu.make_async_copy(e_hbm, e_v, load_sem.at[0])
     m_copy = pltpu.make_async_copy(m_hbm, m_v, load_sem.at[1])
     v_copy = pltpu.make_async_copy(v_hbm, v_v, load_sem.at[2])
+    pltpu.make_async_copy(hid_hbm, hid_s.at[core], near_recv).start()
     e_copy.start()
-    for copy in firsts:
-        copy.wait()
+    for k, src in enumerate((ln_hbm, lm_hbm, lv_hbm)):
+        pltpu.make_async_copy(src, lns_o.at[k], load_sem.at[3]).start()
+    for k, src in enumerate((tgt_hbm, msk_hbm)):
+        pltpu.make_async_copy(src, ids_s.at[core, k], ids_recv).start()
     pl.semaphore_wait(barrier, n - 1)
 
     def send(src, dst, peer, send_sem, recv_sem):
@@ -107,11 +104,14 @@
         copy.start()
         return copy
 
-    gathers = []
-    for k, (src, dst) in enumerate(((hid_ref, hid_s), (tgt_ref, tgt_s), (msk_ref, msk_s))):
-        dst[core] = src[...]
+    def all_of(ref, sem):
+        pltpu.make_async_copy(ref, ref, sem).wait()
+
+    for r in (1, 2, 0):
+        send(hid_hbm, hid_s.at[2 + core if r else core], peers[r], hid_send, far_recv if r else near_recv)
+    for k, src in enumerate((tgt_hbm, msk_hbm)):
         for r, peer in enumerate(peers):
-            gathers.append(send(src, dst.at[2 + core if r else core], peer, in_send.at[k, r], in_recv.at[k, r]))
+            send(src, ids_s.at[2 + core if r else core, k], peer, ids_send, ids_recv)
     xd_s[...] = jnp.zeros(xd_s.shape, BF16)
     e_copy.wait()
     m_copy.start()
@@ -123,7 +123,7 @@
         cent = hid - jnp.mean(hid, axis=-1, keepdims=True)
         rstd = lax.rsqrt(jnp.mean(cent * cent, axis=-1, keepdims=True) + LN_EPS)
         xhat = cent * rstd
-        x_b = (xhat * ln_ref[0:1, :] + ln_ref[1:2, :]).astype(BF16)
+        x_b = (xhat * lns_o[0, 0:1, :] + lns_o[0, 1:2, :]).astype(BF16)
         x_v[lanes, :] = x_b
         x_t = x_b.T
         xd_s[h, 0:dim, 0:wide] = x_t
@@ -154,17 +154,19 @@
         st_tx[0:1, h * wide:(h + 1) * wide] = peak
         st_tx[1:2, h * wide:(h + 1) * wide] = total[:, :wide] + total[:, wide:]
 
-    gathers[0].wait_recv()
+    all_of(lns_o, load_sem.at[3])
+    all_of(hid_s.at[pl.ds(0, 2)], near_recv)
     norm(0)
     forward(0)
-    for copy in gathers[1:]:
-        copy.wait_recv()
+    all_of(hid_s.at[pl.ds(2, 2)], far_recv)
     norm(1)
     forward(1)
-    stats = [send(st_tx, st_rx.at[r], peer, st_send.at[r], st_recv.at[r]) for r, peer in enumerate(peers)]
-
-    tgt = jnp.concatenate([tgt_s[j] for j in range(n)], axis=1)
-    msk = jnp.concatenate([msk_s[j] for j in range(n)], axis=1).astype(F32)
+    for r, peer in enumerate(peers):
+        send(st_tx, st_rx.at[r], peer, st_send, st_recv)
+    all_of(ids_s, ids_recv)
+
+    tgt = jnp.concatenate([ids_s[j, 0] for j in range(n)], axis=1)
+    msk = jnp.concatenate([ids_s[j, 1] for j in range(n)], axis=1).astype(F32)
     count = jnp.sum(msk, axis=1, keepdims=True)
     scale = msk / count
     rel = tgt - me * rows
@@ -198,8 +200,7 @@
     tgt_z = jnp.sum(x_v[...].astype(F32).T * rows_t, axis=0, keepdims=True)
     tgt_z = jnp.where(inside, tgt_z, 0.0)
 
-    for copy in stats:
-        copy.wait_recv()
+    all_of(st_rx, st_recv)
     both = [st_tx[...], st_rx[0], swap(st_rx[1]), swap(st_rx[2])]
     peak = jnp.maximum(jnp.maximum(both[0][0:1], both[1][0:1]), jnp.maximum(both[2][0:1], both[3][0:1]))
     sums = [v[1:2] * jnp.exp2((v[0:1] - peak) * LOG2E) for v in both]
@@ -244,8 +245,10 @@
         mine = pl.ds(pl.multiple_of(c * wide + core * local, local), local)
         out[0:local, :] = dx_s[mine, :] + pk_rx[c, 0:local, :]
         out[local:local + 8, :] = extra + pk_rx[c, local:local + 8, :]
-    for copy in gathers + stats + [part]:
-        copy.wait_send()
+    part.wait_send()
+    all_of(hid_s.at[pl.ds(0, n - 1)], hid_send)
+    all_of(ids_s.at[pl.ds(0, n - 1)], ids_send)
+    all_of(st_rx, st_send)
 
 
 def update_kernel(e_v, m_v, v_v, dz_v, x_v, e_o, m_o, v_o, e_s, m_s, v_s, sem):
@@ -253,25 +256,19 @@
     blocks = row_blocks(rows)
     shift = blocks[EARLY][0]
     outs = (e_o, m_o, v_o)
-    copies = []
-    for b, (base, size) in enumerate(blocks[:EARLY]):
+    for base, size in blocks[:EARLY]:
         for k, src in enumerate((e_v, m_v, v_v)):
-            copy = pltpu.make_async_copy(src.at[pl.ds(base, size)], outs[k].at[pl.ds(base, size)], sem.at[k, b])
-            copy.start()
-            copies.append(copy)
-    for b, (base, size) in enumerate(blocks[EARLY:]):
+            pltpu.make_async_copy(src.at[pl.ds(base, size)], outs[k].at[pl.ds(base, size)], sem.at[k]).start()
+    for base, size in blocks[EARLY:]:
         adam_rows(base, size, e_v, m_v, v_v, dz_v, x_v, e_s, m_s, v_s, shift)
         for k, src in enumerate((e_s, m_s, v_s)):
-            copy = pltpu.make_async_copy(src.at[pl.ds(base - shift, size)], outs[k].at[pl.ds(base, size)],
-                                         sem.at[k, EARLY + b])
-            copy.start()
-            copies.append(copy)
-
-    for copy in copies:
-        copy.wait()
-
-
-def finish_kernel(n, keep_ref, xh_ref, rs_ref, lse_ref, msk_ref, ln_ref, lm_ref, lv_ref, got_ref,
+            pltpu.make_async_copy(
+                src.at[pl.ds(base - shift, size)], outs[k].at[pl.ds(base, size)], sem.at[k]).start()
+    for k, src in enumerate((e_v, m_v, v_v)):
+        pltpu.make_async_copy(src, outs[k], sem.at[k]).wait()
+
+
+def finish_kernel(n, keep_ref, xh_ref, rs_ref, lse_ref, msk_ref, lns_ref, got_ref,
                   tok_o, mean_o, dh_o, ln_o, lmo, lvo):
     _, core, _ = place()
     local, dim = xh_ref.shape
@@ -286,11 +283,11 @@
     mean_o[...] = jnp.sum(loss[:, :wide] + loss[:, wide:], axis=1, keepdims=True) / jnp.sum(msk, axis=1, keepdims=True)
     tok_o[...] = jnp.where(core == 0, loss[:, :local], loss[:, local:wide])
     xhat = xh_ref[...]
-    dxh = dx * ln_ref[0:1, :]
+    dxh = dx * lns_ref[0, 0:1, :]
     dh = rs_ref[...] * (dxh - jnp.mean(dxh, axis=-1, keepdims=True)
                         - xhat * jnp.mean(dxh * xhat, axis=-1, keepdims=True))
     dh_o[...] = dh.astype(BF16)
-    p_new, m_new, v_new = adam(ln_ref[...], extra[0:2], lm_ref[...], lv_ref[...], 0.0)
+    p_new, m_new, v_new = adam(lns_ref[0], extra[0:2], lns_ref[1], lns_ref[2], 0.0)
     ln_o[...] = p_new
     lmo[...] = m_new
     lvo[...] = v_new
@@ -316,7 +313,7 @@
         big = [((rows, dim), BF16), ((rows, dim), F32), ((rows, dim), F32)]
         pack = ((local + 8, dim), F32)
         mid = big + [((rows, toks), BF16), ((toks, dim), BF16), pack, pack, ((local, dim), F32), ((local, dim), F32),
-                     ((1, toks), F32), ((1, toks), F32), ((2, dim), F32), ((2, dim), F32), ((2, dim), F32)]
+                     ((1, toks), F32), ((1, toks), F32), ((3, 2, dim), F32)]
         small = [((1, local), F32), ((1, 1), F32), ((local, dim), BF16), ((2, dim), F32), ((2, dim), F32),
                  ((2, dim), F32)]
         dma = pltpu.SemaphoreType.DMA
@@ -328,15 +325,13 @@
             in_specs=[hbm] * 9,
             out_specs=[vmem] * len(mid),
             scratch_shapes=[
-                pltpu.VMEM((local, dim), BF16), pltpu.VMEM((1, local), jnp.int32), pltpu.VMEM((1, local), jnp.int32),
-                pltpu.VMEM((n, local, dim), BF16), pltpu.VMEM((n, 1, local), jnp.int32),
-                pltpu.VMEM((n, 1, local), jnp.int32), pltpu.VMEM((toks, dim), F32), pltpu.VMEM((toks, dim), F32),
-                pltpu.VMEM((toks, dim), F32),
+                pltpu.VMEM((n, local, dim), BF16), pltpu.VMEM((n, 2, 1, local), jnp.int32),
+                pltpu.VMEM((toks, dim), F32), pltpu.VMEM((toks, dim), F32), pltpu.VMEM((toks, dim), F32),
                 pltpu.VMEM((2, 2 * dim, toks), BF16), pltpu.VMEM((2, half, toks), F32),
                 pltpu.VMEM((2, -(-half // SUB), 8, toks), F32), pltpu.VMEM((dim, -(-rows // 128) * 128), BF16),
                 pltpu.VMEM((2, toks), F32), pltpu.VMEM((peers, 2, toks), F32),
                 pltpu.VMEM((n // 2, local + 8, dim), F32), pltpu.VMEM((n // 2, local + 8, dim), F32),
-                dma((9,)), dma((3, peers)), dma((3, peers)), dma((peers,)), dma((peers,)), dma, dma,
+                dma((4,)), dma, dma, dma, dma, dma, dma, dma, dma, dma,
             ],
             compiler_params=pltpu.CompilerParams(
                 collective_id=0, has_side_effects=True, vmem_limit_bytes=26 << 20),
@@ -352,7 +347,7 @@
             out_specs=[hbm] * 3,
             scratch_shapes=[
                 pltpu.VMEM((late, dim), BF16), pltpu.VMEM((late, dim), F32), pltpu.VMEM((late, dim), F32),
-                dma((3, len(blocks)))],
+                dma((3,))],
             compiler_params=pltpu.CompilerParams(vmem_limit_bytes=20 << 20),
             cost_estimate=pl.CostEstimate(flops=50_000_000_000, bytes_accessed=32_000_000, transcendentals=0),
         )(*[pltpu.with_memory_space_constraint(a, pltpu.VMEM) for a in mids[:5]])
@@ -360,7 +355,7 @@
             functools.partial(finish_kernel, n),
             name="finish",
             out_shape=[jax.ShapeDtypeStruct(*s) for s in small],
-            in_specs=[vmem] * 9,
+            in_specs=[vmem] * 7,
             out_specs=[vmem] * 6,
             compiler_params=pltpu.CompilerParams(vmem_limit_bytes=4 << 20),
         )(mids[5], *mids[7:], got)

time: 22.4 us -> 21.5 us (0.960)
  Pallas kernels: 20.7 us -> 19.8 us
    pallas_call x1, Pallas kernels: 14 us -> 13.5 us  [device_step(): pl.pallas_call(functools.partial(forward_kernel, n), name='forward', out_...]
    pallas_call x1, Pallas kernels: 6.01 us -> 5.58 us  [device_step(): pl.pallas_call(update_kernel, name='update', out_shape=[jax.ShapeDtypeStr...]
  transfers between devices with their start and end apart: 1 -> 1, of which waited for: 0 -> 0; matrix products, arithmetic and copies ran while one was open for 0% -> 0% of each run, Pallas kernels for 27% -> 26%
where the time goes in v5:
time: 21.5 us; the launch traced here: 21.4 us
  Pallas kernels  19.8 us (92%)
  starting transfers between devices  0.89 us (4%)
  between operations  0.67 us (3%)
    pallas_call x1, Pallas kernels, device_step(): pl.pallas_call(functools.partial(forward_kernel, n), name='forward', out_...  13.5 us
    pallas_call x1, Pallas kernels, device_step(): pl.pallas_call(update_kernel, name='update', out_shape=[jax.ShapeDtypeStr...  5.58 us
    ppermute x1, starting transfers between devices, device_step(): got = lax.ppermute(mids[6], 'tp', [(i, (i + n // 2) % n) for i in range(n)])  0.89 us
    pallas_call x1, Pallas kernels, device_step(): pl.pallas_call(functools.partial(finish_kernel, n), name='finish', out_sh...  0.72 us
  transfers between devices with their start and end apart: 1, of which 0 were waited for; matrix products, arithmetic and copies ran while one was open for 0% of the time, Pallas kernels for 26%

profile of v5, /device:TPU:0, one launch (start us, length us, event | category | flops | bytes accessed | tf_op | source)
XLA Modules:
  0.0 21.4 jit_solution(4742463567436528172)
XLA Ops:
  0.6 13.5 %forward.1 = (bf16[12576,128]{1,0:T(8,128)(2,1)S(1)}, f32[12576,128]{1,0:T(8,128)S(1)}, f32[12576,128]{1,0:T(8,128)S(1)}, bf16[12576,256]{1,0:T(8,128)(2,1)S(1)}...) custom-call(bf16[64,128]{1,0:T(8,128)(2,1)} %hid_hbm.1, ...), custom_call_target="tpu_custom_call" | custom-call | tf_op jit(solution)/shard_map/forward/pallas_call | solution.py:321
  14.2 0.9 %collective-permute-start = (f32[72,128]{1,0:T(8,128)S(1)}, f32[72,128]{1,0:T(8,128)S(1)}, u32[]{:S(2)}, u32[]{:S(2)}) collective-permute-start(f32[72,128]{1,0:T(8,128)S(1)} %get-tuple-element.36), channel_id=1, source_target_pairs={{0,2},{1,3},{2,0},{3,1},{4,6},{5,7},{6,4},{7,5}} | collective-permute-start | bytes 110600 | tf_op jit(solution)/shard_map/ppermute | solution.py:341
  15.1 5.6 %update.1 = (bf16[12576,128]{1,0:T(8,128)(2,1)}, f32[12576,128]{1,0:T(8,128)}, f32[12576,128]{1,0:T(8,128)}) custom-call(bf16[12576,128]{1,0:T(8,128)(2,1)S(1)} %get-tuple-element.43.e_v, f32[12576,128]{1,0:T(8,128)S(1)} %get-tuple-element.44.m_v, f32[12576,128]{1,0:T(8,128)S(1)} %get-tuple-element.45.v_v, bf16[12576,256]{1,0:T(8,128)(2,1)S(1)} %get-tuple-element.46.dz_v, ...), custom_call_target="tpu_custom_call" | custom-call | flops 49999998976 | bytes 32000000 | tf_op jit(solution)/shard_map/update/pallas_call | solution.py:342
  20.7 0.0 collective-permute-done.got_ref
  20.7 0.7 %finish.1 = (f32[1,64]{1,0:T(1,128)}, f32[1,1]{1,0:T(1,128)}, bf16[64,128]{1,0:T(8,128)(2,1)}, f32[2,128]{1,0:T(2,128)}, f32[2,128]{1,0:T(2,128)}, /*index=5*/f32[2,128]{1,0:T(2,128)}) custom-call(f32[72,128]{1,0:T(8,128)S(1)} %get-tuple-element.30.keep_ref, f32[64,128]{1,0:T(8,128)S(1)} %get-tuple-element.31.xh_ref, ...), custom_call_target="tpu_custom_call" | custom-call | tf_op jit(solution)/shard_map/finish/pallas_call | solution.py:354
Async XLA Ops:
  14.2 6.5 %collective-permute-start = (f32[72,128]{1,0:T(8,128)S(1)}, f32[72,128]{1,0:T(8,128)S(1)}, u32[]{:S(2)}, u32[]{:S(2)}) collective-permute-start(f32[72,128]{1,0:T(8,128)S(1)} %get-tuple-element.36), channel_id=1, source_target_pairs={{0,2},{1,3},{2,0},{3,1},{4,6},{5,7},{6,4},{7,5}} | collective-permute-start | bytes 110600 | tf_op jit(solution)/shard_map/ppermute | solution.py:341

commit v6 on v5

--- a/solution.py
+++ b/solution.py
@@ -17,8 +17,8 @@
 LOG2E = 1.4426950408889634
 TINY = 1e-37
 SUB = 128
-CHUNK = 448
-EARLY = 4
+CHUNK = 256
+EARLY = 7
 DOT = 896
 MESH = pl.DeviceIdType.MESH
 F32 = jnp.float32
@@ -144,7 +144,7 @@
                 new = jnp.maximum(top, jnp.max(zk, axis=0))
                 ek = jnp.exp2((zk - new[None]) * LOG2E)
                 ebuf[h, pl.ds(first + k, size), :] = ek.reshape(size, toks)
-                mbuf[h, (first + k) // SUB] = new
+                mbuf[h, (first + k) // SUB] = new * LOG2E
                 total = total * jnp.exp2((top - new) * LOG2E) + jnp.sum(ek, axis=0)
                 top = new
         peak = jnp.max(top, axis=0, keepdims=True)
@@ -205,6 +205,7 @@
     peak = jnp.maximum(jnp.maximum(both[0][0:1], both[1][0:1]), jnp.maximum(both[2][0:1], both[3][0:1]))
     sums = [v[1:2] * jnp.exp2((v[0:1] - peak) * LOG2E) for v in both]
     lse = peak + jnp.log((sums[0] + sums[1]) + (sums[2] + sums[3]))
+    shift = jnp.broadcast_to(lse * LOG2E - jnp.log2(scale), (8, toks))
     hot_val = (jnp.exp2((tgt_z - lse) * LOG2E) - 1.0) * scale
     hot16 = jnp.broadcast_to(hot_val, (16, toks)).astype(BF16)[None]
 
@@ -212,7 +213,7 @@
         h, first = low // half, low % half
         sides = slice(h * wide, (h + 1) * wide)
         seen = jnp.concatenate([mbuf[c, first // SUB, :, sides] for c in range(2)], axis=1)
-        fac = jnp.exp2((seen - lse) * LOG2E) * scale
+        fac = jnp.exp2(seen - shift)
         ek = jnp.concatenate([ebuf[c, pl.ds(first, size), sides] for c in range(2)], axis=1)
         dz = (ek.reshape(size // 8, 8, toks) * fac[None]).reshape(size // 16, 16, toks).astype(BF16)
         dz = jnp.where(hit(low, size), hot16, dz).reshape(size, toks)

time: 21.5 us -> 21.3 us (level)
  no operation moved by 1% of the time
where the time goes in v6:
time: 21.3 us; the launch traced here: 21.2 us
  Pallas kernels  19.6 us (92%)
  starting transfers between devices  0.92 us (4%)
  between operations  0.67 us (3%)
    pallas_call x1, Pallas kernels, device_step(): pl.pallas_call(functools.partial(forward_kernel, n), name='forward', out_...  13.4 us
    pallas_call x1, Pallas kernels, device_step(): pl.pallas_call(update_kernel, name='update', out_shape=[jax.ShapeDtypeStr...  5.53 us
    ppermute x1, starting transfers between devices, device_step(): got = lax.ppermute(mids[6], 'tp', [(i, (i + n // 2) % n) for i in range(n)])  0.92 us
    pallas_call x1, Pallas kernels, device_step(): pl.pallas_call(functools.partial(finish_kernel, n), name='finish', out_sh...  0.72 us
  transfers between devices with their start and end apart: 1, of which 0 were waited for; matrix products, arithmetic and copies ran while one was open for 0% of the time, Pallas kernels for 26%

profile of v6, /device:TPU:0, one launch (start us, length us, event | category | flops | bytes accessed | tf_op | source)
XLA Modules:
  0.0 21.2 jit_solution(10399545965522857589)
XLA Ops:
  0.6 13.4 %forward.1 = (bf16[12576,128]{1,0:T(8,128)(2,1)S(1)}, f32[12576,128]{1,0:T(8,128)S(1)}, f32[12576,128]{1,0:T(8,128)S(1)}, bf16[12576,256]{1,0:T(8,128)(2,1)S(1)}...) custom-call(bf16[64,128]{1,0:T(8,128)(2,1)} %hid_hbm.1, ...), custom_call_target="tpu_custom_call" | custom-call | tf_op jit(solution)/shard_map/forward/pallas_call | solution.py:322
  14.0 0.9 %collective-permute-start = (f32[72,128]{1,0:T(8,128)S(1)}, f32[72,128]{1,0:T(8,128)S(1)}, u32[]{:S(2)}, u32[]{:S(2)}) collective-permute-start(f32[72,128]{1,0:T(8,128)S(1)} %get-tuple-element.36), channel_id=1, source_target_pairs={{0,2},{1,3},{2,0},{3,1},{4,6},{5,7},{6,4},{7,5}} | collective-permute-start | bytes 110600 | tf_op jit(solution)/shard_map/ppermute | solution.py:342
  14.9 5.5 %update.1 = (bf16[12576,128]{1,0:T(8,128)(2,1)}, f32[12576,128]{1,0:T(8,128)}, f32[12576,128]{1,0:T(8,128)}) custom-call(bf16[12576,128]{1,0:T(8,128)(2,1)S(1)} %get-tuple-element.43.e_v, f32[12576,128]{1,0:T(8,128)S(1)} %get-tuple-element.44.m_v, f32[12576,128]{1,0:T(8,128)S(1)} %get-tuple-element.45.v_v, bf16[12576,256]{1,0:T(8,128)(2,1)S(1)} %get-tuple-element.46.dz_v, ...), custom_call_target="tpu_custom_call" | custom-call | flops 49999998976 | bytes 32000000 | tf_op jit(solution)/shard_map/update/pallas_call | solution.py:343
  20.5 0.0 collective-permute-done.got_ref
  20.5 0.7 %finish.1 = (f32[1,64]{1,0:T(1,128)}, f32[1,1]{1,0:T(1,128)}, bf16[64,128]{1,0:T(8,128)(2,1)}, f32[2,128]{1,0:T(2,128)}, f32[2,128]{1,0:T(2,128)}, /*index=5*/f32[2,128]{1,0:T(2,128)}) custom-call(f32[72,128]{1,0:T(8,128)S(1)} %get-tuple-element.30.keep_ref, f32[64,128]{1,0:T(8,128)S(1)} %get-tuple-element.31.xh_ref, ...), custom_call_target="tpu_custom_call" | custom-call | tf_op jit(solution)/shard_map/finish/pallas_call | solution.py:355
Async XLA Ops:
  14.0 6.5 %collective-permute-start = (f32[72,128]{1,0:T(8,128)S(1)}, f32[72,128]{1,0:T(8,128)S(1)}, u32[]{:S(2)}, u32[]{:S(2)}) collective-permute-start(f32[72,128]{1,0:T(8,128)S(1)} %get-tuple-element.36), channel_id=1, source_target_pairs={{0,2},{1,3},{2,0},{3,1},{4,6},{5,7},{6,4},{7,5}} | collective-permute-start | bytes 110600 | tf_op jit(solution)/shard_map/ppermute | solution.py:342

commit v7 on v6

--- a/solution.py
+++ b/solution.py
@@ -197,7 +197,9 @@
 
     ones, none = jnp.ones((1, 16, toks), BF16), jnp.zeros((1, 16, toks), BF16)
     rows_t = gather_sum(lambda low, size: jnp.where(hit(low, size), ones, none).reshape(size, toks))
-    tgt_z = jnp.sum(x_v[...].astype(F32).T * rows_t, axis=0, keepdims=True)
+    cross = jnp.dot(x_v[...], rows_t.astype(BF16), preferred_element_type=F32)
+    diag = lax.broadcasted_iota(jnp.int32, (toks, toks), 0) == lax.broadcasted_iota(jnp.int32, (toks, toks), 1)
+    tgt_z = jnp.sum(jnp.where(diag, cross, 0.0), axis=0, keepdims=True)
     tgt_z = jnp.where(inside, tgt_z, 0.0)
 
     all_of(st_rx, st_recv)

time: 21.3 us -> 21.3 us (level)
  no operation moved by 1% of the time
where the time goes in v7:
time: 21.3 us; the launch traced here: 21.2 us
  Pallas kernels  19.6 us (92%)
  starting transfers between devices  0.87 us (4%)
  between operations  0.67 us (3%)
    pallas_call x1, Pallas kernels, device_step(): pl.pallas_call(functools.partial(forward_kernel, n), name='forward', out_...  13.4 us
    pallas_call x1, Pallas kernels, device_step(): pl.pallas_call(update_kernel, name='update', out_shape=[jax.ShapeDtypeStr...  5.53 us
    ppermute x1, starting transfers between devices, device_step(): got = lax.ppermute(mids[6], 'tp', [(i, (i + n // 2) % n) for i in range(n)])  0.87 us
    pallas_call x1, Pallas kernels, device_step(): pl.pallas_call(functools.partial(finish_kernel, n), name='finish', out_sh...  0.72 us
  transfers between devices with their start and end apart: 1, of which 0 were waited for; matrix products, arithmetic and copies ran while one was open for 0% of the time, Pallas kernels for 26%

profile of v7, /device:TPU:0, one launch (start us, length us, event | category | flops | bytes accessed | tf_op | source)
XLA Modules:
  0.0 21.2 jit_solution(1727359885124015519)
XLA Ops:
  0.6 13.4 %forward.1 = (bf16[12576,128]{1,0:T(8,128)(2,1)S(1)}, f32[12576,128]{1,0:T(8,128)S(1)}, f32[12576,128]{1,0:T(8,128)S(1)}, bf16[12576,256]{1,0:T(8,128)(2,1)S(1)}...) custom-call(bf16[64,128]{1,0:T(8,128)(2,1)} %hid_hbm.1, ...), custom_call_target="tpu_custom_call" | custom-call | tf_op jit(solution)/shard_map/forward/pallas_call | solution.py:324
  14.0 0.9 %collective-permute-start = (f32[72,128]{1,0:T(8,128)S(1)}, f32[72,128]{1,0:T(8,128)S(1)}, u32[]{:S(2)}, u32[]{:S(2)}) collective-permute-start(f32[72,128]{1,0:T(8,128)S(1)} %get-tuple-element.36), channel_id=1, source_target_pairs={{0,2},{1,3},{2,0},{3,1},{4,6},{5,7},{6,4},{7,5}} | collective-permute-start | bytes 110600 | tf_op jit(solution)/shard_map/ppermute | solution.py:344
  14.9 5.5 %update.1 = (bf16[12576,128]{1,0:T(8,128)(2,1)}, f32[12576,128]{1,0:T(8,128)}, f32[12576,128]{1,0:T(8,128)}) custom-call(bf16[12576,128]{1,0:T(8,128)(2,1)S(1)} %get-tuple-element.43.e_v, f32[12576,128]{1,0:T(8,128)S(1)} %get-tuple-element.44.m_v, f32[12576,128]{1,0:T(8,128)S(1)} %get-tuple-element.45.v_v, bf16[12576,256]{1,0:T(8,128)(2,1)S(1)} %get-tuple-element.46.dz_v, ...), custom_call_target="tpu_custom_call" | custom-call | flops 49999998976 | bytes 32000000 | tf_op jit(solution)/shard_map/update/pallas_call | solution.py:345
  20.4 0.0 collective-permute-done.got_ref
  20.4 0.7 %finish.1 = (f32[1,64]{1,0:T(1,128)}, f32[1,1]{1,0:T(1,128)}, bf16[64,128]{1,0:T(8,128)(2,1)}, f32[2,128]{1,0:T(2,128)}, f32[2,128]{1,0:T(2,128)}, /*index=5*/f32[2,128]{1,0:T(2,128)}) custom-call(f32[72,128]{1,0:T(8,128)S(1)} %get-tuple-element.30.keep_ref, f32[64,128]{1,0:T(8,128)S(1)} %get-tuple-element.31.xh_ref, ...), custom_call_target="tpu_custom_call" | custom-call | tf_op jit(solution)/shard_map/finish/pallas_call | solution.py:357
Async XLA Ops:
  14.0 6.4 %collective-permute-start = (f32[72,128]{1,0:T(8,128)S(1)}, f32[72,128]{1,0:T(8,128)S(1)}, u32[]{:S(2)}, u32[]{:S(2)}) collective-permute-start(f32[72,128]{1,0:T(8,128)S(1)} %get-tuple-element.36), channel_id=1, source_target_pairs={{0,2},{1,3},{2,0},{3,1},{4,6},{5,7},{6,4},{7,5}} | collective-permute-start | bytes 110600 | tf_op jit(solution)/shard_map/ppermute | solution.py:344

commit v8 on v7

--- a/solution.py
+++ b/solution.py
@@ -17,8 +17,8 @@
 LOG2E = 1.4426950408889634
 TINY = 1e-37
 SUB = 128
-CHUNK = 256
-EARLY = 7
+CHUNK = 128
+EARLY = 14
 DOT = 896
 MESH = pl.DeviceIdType.MESH
 F32 = jnp.float32

time: 21.3 us -> 21.2 us (level)
  no operation moved by 1% of the time
where the time goes in v8:
time: 21.2 us; the launch traced here: 21.1 us
  Pallas kernels  19.6 us (92%)
  starting transfers between devices  0.87 us (4%)
  between operations  0.67 us (3%)
    pallas_call x1, Pallas kernels, device_step(): pl.pallas_call(functools.partial(forward_kernel, n), name='forward', out_...  13.4 us
    pallas_call x1, Pallas kernels, device_step(): pl.pallas_call(update_kernel, name='update', out_shape=[jax.ShapeDtypeStr...  5.49 us
    ppermute x1, starting transfers between devices, device_step(): got = lax.ppermute(mids[6], 'tp', [(i, (i + n // 2) % n) for i in range(n)])  0.87 us
    pallas_call x1, Pallas kernels, device_step(): pl.pallas_call(functools.partial(finish_kernel, n), name='finish', out_sh...  0.72 us
  transfers between devices with their start and end apart: 1, of which 0 were waited for; matrix products, arithmetic and copies ran while one was open for 0% of the time, Pallas kernels for 26%

profile of v8, /device:TPU:0, one launch (start us, length us, event | category | flops | bytes accessed | tf_op | source)
XLA Modules:
  0.0 21.1 jit_solution(1412465322067455316)
XLA Ops:
  0.6 13.4 %forward.1 = (bf16[12576,128]{1,0:T(8,128)(2,1)S(1)}, f32[12576,128]{1,0:T(8,128)S(1)}, f32[12576,128]{1,0:T(8,128)S(1)}, bf16[12576,256]{1,0:T(8,128)(2,1)S(1)}...) custom-call(bf16[64,128]{1,0:T(8,128)(2,1)} %hid_hbm.1, ...), custom_call_target="tpu_custom_call" | custom-call | tf_op jit(solution)/shard_map/forward/pallas_call | solution.py:324
  14.0 0.9 %collective-permute-start = (f32[72,128]{1,0:T(8,128)S(1)}, f32[72,128]{1,0:T(8,128)S(1)}, u32[]{:S(2)}, u32[]{:S(2)}) collective-permute-start(f32[72,128]{1,0:T(8,128)S(1)} %get-tuple-element.36), channel_id=1, source_target_pairs={{0,2},{1,3},{2,0},{3,1},{4,6},{5,7},{6,4},{7,5}} | collective-permute-start | bytes 110600 | tf_op jit(solution)/shard_map/ppermute | solution.py:344
  14.9 5.5 %update.1 = (bf16[12576,128]{1,0:T(8,128)(2,1)}, f32[12576,128]{1,0:T(8,128)}, f32[12576,128]{1,0:T(8,128)}) custom-call(bf16[12576,128]{1,0:T(8,128)(2,1)S(1)} %get-tuple-element.43.e_v, f32[12576,128]{1,0:T(8,128)S(1)} %get-tuple-element.44.m_v, f32[12576,128]{1,0:T(8,128)S(1)} %get-tuple-element.45.v_v, bf16[12576,256]{1,0:T(8,128)(2,1)S(1)} %get-tuple-element.46.dz_v, ...), custom_call_target="tpu_custom_call" | custom-call | flops 49999998976 | bytes 32000000 | tf_op jit(solution)/shard_map/update/pallas_call | solution.py:345
  20.4 0.0 collective-permute-done.got_ref
  20.4 0.7 %finish.1 = (f32[1,64]{1,0:T(1,128)}, f32[1,1]{1,0:T(1,128)}, bf16[64,128]{1,0:T(8,128)(2,1)}, f32[2,128]{1,0:T(2,128)}, f32[2,128]{1,0:T(2,128)}, /*index=5*/f32[2,128]{1,0:T(2,128)}) custom-call(f32[72,128]{1,0:T(8,128)S(1)} %get-tuple-element.30.keep_ref, f32[64,128]{1,0:T(8,128)S(1)} %get-tuple-element.31.xh_ref, ...), custom_call_target="tpu_custom_call" | custom-call | tf_op jit(solution)/shard_map/finish/pallas_call | solution.py:357
Async XLA Ops:
  14.0 6.4 %collective-permute-start = (f32[72,128]{1,0:T(8,128)S(1)}, f32[72,128]{1,0:T(8,128)S(1)}, u32[]{:S(2)}, u32[]{:S(2)}) collective-permute-start(f32[72,128]{1,0:T(8,128)S(1)} %get-tuple-element.36), channel_id=1, source_target_pairs={{0,2},{1,3},{2,0},{3,1},{4,6},{5,7},{6,4},{7,5}} | collective-permute-start | bytes 110600 | tf_op jit(solution)/shard_map/ppermute | solution.py:344

commit v9 on v8

--- a/solution.py
+++ b/solution.py
@@ -125,9 +125,8 @@
         xhat = cent * rstd
         x_b = (xhat * lns_o[0, 0:1, :] + lns_o[0, 1:2, :]).astype(BF16)
         x_v[lanes, :] = x_b
-        x_t = x_b.T
-        xd_s[h, 0:dim, 0:wide] = x_t
-        xd_s[h, dim:2 * dim, wide:2 * wide] = x_t
+        xd_s[h, 0:wide, 0:dim] = x_b
+        xd_s[h, wide:2 * wide, dim:2 * dim] = x_b
         xhat_s[lanes, :] = xhat
         rstd_s[lanes, :] = jnp.broadcast_to(rstd, (wide, dim))
 
@@ -137,7 +136,7 @@
         for first in range(0, half, DOT):
             span = min(DOT, half - first)
             pair = jnp.concatenate([e_v[pl.ds(first, span), :], e_v[pl.ds(half + first, span), :]], axis=1)
-            z = jnp.dot(pair, xd_s[h], preferred_element_type=F32)
+            z = lax.dot_general(pair, xd_s[h], (((1,), (1,)), ((), ())), preferred_element_type=F32)
             for k in range(0, span, SUB):
                 size = min(SUB, span - k)
                 zk = z[k:k + size].reshape(size // 8, 8, toks)
@@ -161,8 +160,8 @@
     all_of(hid_s.at[pl.ds(2, 2)], far_recv)
     norm(1)
     forward(1)
-    for r, peer in enumerate(peers):
-        send(st_tx, st_rx.at[r], peer, st_send, st_recv)
+    for r in (1, 2, 0):
+        send(st_tx, st_rx.at[r], peers[r], st_send, st_recv)
     all_of(ids_s, ids_recv)
 
     tgt = jnp.concatenate([ids_s[j, 0] for j in range(n)], axis=1)
@@ -181,8 +180,10 @@
     flat = jnp.zeros((16, toks), jnp.int32)
     iota16 = lax.broadcasted_iota(jnp.int32, (SUB, toks), 0).astype(jnp.int16).reshape(SUB // 16, 16, toks)
 
+    near16 = (flat + near).astype(jnp.int16)
+
     def hit(low, size):
-        return iota16[:size // 16] == (flat + (near - low)).astype(jnp.int16)[None]
+        return iota16[:size // 16] == (near16 - jnp.int16(low))[None]
 
     def gather_sum(value):
         accs = [jnp.zeros((dim, toks), F32)] * 2
@@ -330,7 +331,7 @@
             scratch_shapes=[
                 pltpu.VMEM((n, local, dim), BF16), pltpu.VMEM((n, 2, 1, local), jnp.int32),
                 pltpu.VMEM((toks, dim), F32), pltpu.VMEM((toks, dim), F32), pltpu.VMEM((toks, dim), F32),
-                pltpu.VMEM((2, 2 * dim, toks), BF16), pltpu.VMEM((2, half, toks), F32),
+                pltpu.VMEM((2, toks, 2 * dim), BF16), pltpu.VMEM((2, half, toks), F32),
                 pltpu.VMEM((2, -(-half // SUB), 8, toks), F32), pltpu.VMEM((dim, -(-rows // 128) * 128), BF16),
                 pltpu.VMEM((2, toks), F32), pltpu.VMEM((peers, 2, toks), F32),
                 pltpu.VMEM((n // 2, local + 8, dim), F32), pltpu.VMEM((n // 2, local + 8, dim), F32),

time: 21.2 us -> 21.2 us (level)
  no operation moved by 1% of the time
where the time goes in v9:
time: 21.2 us; the launch traced here: 21.1 us
  Pallas kernels  19.5 us (92%)
  starting transfers between devices  0.86 us (4%)
  between operations  0.67 us (3%)
    pallas_call x1, Pallas kernels, device_step(): pl.pallas_call(functools.partial(forward_kernel, n), name='forward', out_...  13.3 us
    pallas_call x1, Pallas kernels, device_step(): pl.pallas_call(update_kernel, name='update', out_shape=[jax.ShapeDtypeStr...  5.49 us
    ppermute x1, starting transfers between devices, device_step(): got = lax.ppermute(mids[6], 'tp', [(i, (i + n // 2) % n) for i in range(n)])  0.86 us
    pallas_call x1, Pallas kernels, device_step(): pl.pallas_call(functools.partial(finish_kernel, n), name='finish', out_sh...  0.72 us
  transfers between devices with their start and end apart: 1, of which 0 were waited for; matrix products, arithmetic and copies ran while one was open for 0% of the time, Pallas kernels for 26%

profile of v9, /device:TPU:0, one launch (start us, length us, event | category | flops | bytes accessed | tf_op | source)
XLA Modules:
  0.0 21.1 jit_solution(1560944757153903029)
XLA Ops:
  0.6 13.3 %forward.1 = (bf16[12576,128]{1,0:T(8,128)(2,1)S(1)}, f32[12576,128]{1,0:T(8,128)S(1)}, f32[12576,128]{1,0:T(8,128)S(1)}, bf16[12576,256]{1,0:T(8,128)(2,1)S(1)}...) custom-call(bf16[64,128]{1,0:T(8,128)(2,1)} %hid_hbm.1, ...), custom_call_target="tpu_custom_call" | custom-call | tf_op jit(solution)/shard_map/forward/pallas_call | solution.py:325
  14.0 0.9 %collective-permute-start = (f32[72,128]{1,0:T(8,128)S(1)}, f32[72,128]{1,0:T(8,128)S(1)}, u32[]{:S(2)}, u32[]{:S(2)}) collective-permute-start(f32[72,128]{1,0:T(8,128)S(1)} %get-tuple-element.36), channel_id=1, source_target_pairs={{0,2},{1,3},{2,0},{3,1},{4,6},{5,7},{6,4},{7,5}} | collective-permute-start | bytes 110600 | tf_op jit(solution)/shard_map/ppermute | solution.py:345
  14.8 5.5 %update.1 = (bf16[12576,128]{1,0:T(8,128)(2,1)}, f32[12576,128]{1,0:T(8,128)}, f32[12576,128]{1,0:T(8,128)}) custom-call(bf16[12576,128]{1,0:T(8,128)(2,1)S(1)} %get-tuple-element.43.e_v, f32[12576,128]{1,0:T(8,128)S(1)} %get-tuple-element.44.m_v, f32[12576,128]{1,0:T(8,128)S(1)} %get-tuple-element.45.v_v, bf16[12576,256]{1,0:T(8,128)(2,1)S(1)} %get-tuple-element.46.dz_v, ...), custom_call_target="tpu_custom_call" | custom-call | flops 49999998976 | bytes 32000000 | tf_op jit(solution)/shard_map/update/pallas_call | solution.py:346
  20.3 0.0 collective-permute-done.got_ref
  20.4 0.7 %finish.1 = (f32[1,64]{1,0:T(1,128)}, f32[1,1]{1,0:T(1,128)}, bf16[64,128]{1,0:T(8,128)(2,1)}, f32[2,128]{1,0:T(2,128)}, f32[2,128]{1,0:T(2,128)}, /*index=5*/f32[2,128]{1,0:T(2,128)}) custom-call(f32[72,128]{1,0:T(8,128)S(1)} %get-tuple-element.30.keep_ref, f32[64,128]{1,0:T(8,128)S(1)} %get-tuple-element.31.xh_ref, ...), custom_call_target="tpu_custom_call" | custom-call | tf_op jit(solution)/shard_map/finish/pallas_call | solution.py:358
Async XLA Ops:
  14.0 6.4 %collective-permute-start = (f32[72,128]{1,0:T(8,128)S(1)}, f32[72,128]{1,0:T(8,128)S(1)}, u32[]{:S(2)}, u32[]{:S(2)}) collective-permute-start(f32[72,128]{1,0:T(8,128)S(1)} %get-tuple-element.36), channel_id=1, source_target_pairs={{0,2},{1,3},{2,0},{3,1},{4,6},{5,7},{6,4},{7,5}} | collective-permute-start | bytes 110600 | tf_op jit(solution)/shard_map/ppermute | solution.py:345

commit v10 on v9

--- a/solution.py
+++ b/solution.py
@@ -19,7 +19,7 @@
 SUB = 128
 CHUNK = 128
 EARLY = 14
-DOT = 896
+DOT = 1792
 MESH = pl.DeviceIdType.MESH
 F32 = jnp.float32
 BF16 = jnp.bfloat16
@@ -89,11 +89,11 @@
         pl.semaphore_signal(barrier, inc=1, device_id={"tp": peer}, device_id_type=MESH)
     e_copy = pltpu.make_async_copy(e_hbm, e_v, load_sem.at[0])
     m_copy = pltpu.make_async_copy(m_hbm, m_v, load_sem.at[1])
-    v_copy = pltpu.make_async_copy(v_hbm, v_v, load_sem.at[2])
+    v_copy = pltpu.make_async_copy(v_hbm, v_v, load_sem.at[1])
     pltpu.make_async_copy(hid_hbm, hid_s.at[core], near_recv).start()
     e_copy.start()
     for k, src in enumerate((ln_hbm, lm_hbm, lv_hbm)):
-        pltpu.make_async_copy(src, lns_o.at[k], load_sem.at[3]).start()
+        pltpu.make_async_copy(src, lns_o.at[k], load_sem.at[2]).start()
     for k, src in enumerate((tgt_hbm, msk_hbm)):
         pltpu.make_async_copy(src, ids_s.at[core, k], ids_recv).start()
     pl.semaphore_wait(barrier, n - 1)
@@ -153,7 +153,7 @@
         st_tx[0:1, h * wide:(h + 1) * wide] = peak
         st_tx[1:2, h * wide:(h + 1) * wide] = total[:, :wide] + total[:, wide:]
 
-    all_of(lns_o, load_sem.at[3])
+    all_of(lns_o, load_sem.at[2])
     all_of(hid_s.at[pl.ds(0, 2)], near_recv)
     norm(0)
     forward(0)
@@ -239,8 +239,7 @@
     rs_o[...] = rstd_s[own, :]
     msk_o[...] = msk
     lse_o[...] = lse
-    m_copy.wait()
-    v_copy.wait()
+    all_of(ebuf, load_sem.at[1])
     for base, size in row_blocks(rows)[:EARLY]:
         adam_rows(base, size, e_v, m_v, v_v, dz_v, x_v, e_v, m_v, v_v, 0)
 
@@ -335,7 +334,7 @@
                 pltpu.VMEM((2, -(-half // SUB), 8, toks), F32), pltpu.VMEM((dim, -(-rows // 128) * 128), BF16),
                 pltpu.VMEM((2, toks), F32), pltpu.VMEM((peers, 2, toks), F32),
                 pltpu.VMEM((n // 2, local + 8, dim), F32), pltpu.VMEM((n // 2, local + 8, dim), F32),
-                dma((4,)), dma, dma, dma, dma, dma, dma, dma, dma, dma,
+                dma((3,)), dma, dma, dma, dma, dma, dma, dma, dma, dma,
             ],
             compiler_params=pltpu.CompilerParams(
                 collective_id=0, has_side_effects=True, vmem_limit_bytes=26 << 20),

time: 21.2 us -> 21.2 us (level)
  no operation moved by 1% of the time
where the time goes in v10:
time: 21.2 us; the launch traced here: 21.1 us
  Pallas kernels  19.5 us (92%)
  starting transfers between devices  0.86 us (4%)
  between operations  0.67 us (3%)
    pallas_call x1, Pallas kernels, device_step(): pl.pallas_call(functools.partial(forward_kernel, n), name='forward', out_...  13.3 us
    pallas_call x1, Pallas kernels, device_step(): pl.pallas_call(update_kernel, name='update', out_shape=[jax.ShapeDtypeStr...  5.49 us
    ppermute x1, starting transfers between devices, device_step(): got = lax.ppermute(mids[6], 'tp', [(i, (i + n // 2) % n) for i in range(n)])  0.86 us
    pallas_call x1, Pallas kernels, device_step(): pl.pallas_call(functools.partial(finish_kernel, n), name='finish', out_sh...  0.72 us
  transfers between devices with their start and end apart: 1, of which 0 were waited for; matrix products, arithmetic and copies ran while one was open for 0% of the time, Pallas kernels for 26%

profile of v10, /device:TPU:0, one launch (start us, length us, event | category | flops | bytes accessed | tf_op | source)
XLA Modules:
  0.0 21.1 jit_solution(12877962147965112682)
XLA Ops:
  0.6 13.3 %forward.1 = (bf16[12576,128]{1,0:T(8,128)(2,1)S(1)}, f32[12576,128]{1,0:T(8,128)S(1)}, f32[12576,128]{1,0:T(8,128)S(1)}, bf16[12576,256]{1,0:T(8,128)(2,1)S(1)}...) custom-call(bf16[64,128]{1,0:T(8,128)(2,1)} %hid_hbm.1, ...), custom_call_target="tpu_custom_call" | custom-call | tf_op jit(solution)/shard_map/forward/pallas_call | solution.py:324
  14.0 0.9 %collective-permute-start = (f32[72,128]{1,0:T(8,128)S(1)}, f32[72,128]{1,0:T(8,128)S(1)}, u32[]{:S(2)}, u32[]{:S(2)}) collective-permute-start(f32[72,128]{1,0:T(8,128)S(1)} %get-tuple-element.36), channel_id=1, source_target_pairs={{0,2},{1,3},{2,0},{3,1},{4,6},{5,7},{6,4},{7,5}} | collective-permute-start | bytes 110600 | tf_op jit(solution)/shard_map/ppermute | solution.py:344
  14.8 5.5 %update.1 = (bf16[12576,128]{1,0:T(8,128)(2,1)}, f32[12576,128]{1,0:T(8,128)}, f32[12576,128]{1,0:T(8,128)}) custom-call(bf16[12576,128]{1,0:T(8,128)(2,1)S(1)} %get-tuple-element.43.e_v, f32[12576,128]{1,0:T(8,128)S(1)} %get-tuple-element.44.m_v, f32[12576,128]{1,0:T(8,128)S(1)} %get-tuple-element.45.v_v, bf16[12576,256]{1,0:T(8,128)(2,1)S(1)} %get-tuple-element.46.dz_v, ...), custom_call_target="tpu_custom_call" | custom-call | flops 49999998976 | bytes 32000000 | tf_op jit(solution)/shard_map/update/pallas_call | solution.py:345
  20.3 0.0 collective-permute-done.got_ref
  20.3 0.7 %finish.1 = (f32[1,64]{1,0:T(1,128)}, f32[1,1]{1,0:T(1,128)}, bf16[64,128]{1,0:T(8,128)(2,1)}, f32[2,128]{1,0:T(2,128)}, f32[2,128]{1,0:T(2,128)}, /*index=5*/f32[2,128]{1,0:T(2,128)}) custom-call(f32[72,128]{1,0:T(8,128)S(1)} %get-tuple-element.30.keep_ref, f32[64,128]{1,0:T(8,128)S(1)} %get-tuple-element.31.xh_ref, ...), custom_call_target="tpu_custom_call" | custom-call | tf_op jit(solution)/shard_map/finish/pallas_call | solution.py:357
Async XLA Ops:
  14.0 6.4 %collective-permute-start = (f32[72,128]{1,0:T(8,128)S(1)}, f32[72,128]{1,0:T(8,128)S(1)}, u32[]{:S(2)}, u32[]{:S(2)}) collective-permute-start(f32[72,128]{1,0:T(8,128)S(1)} %get-tuple-element.36), channel_id=1, source_target_pairs={{0,2},{1,3},{2,0},{3,1},{4,6},{5,7},{6,4},{7,5}} | collective-permute-start | bytes 110600 | tf_op jit(solution)/shard_map/ppermute | solution.py:344
